TPU v7x, 512 devices: a 4x2x32 block of a 4x8x32 slice. The times are simulated.
512 devices in a mesh: groups: 2 (over y), gx: 32 (over z), gy: 4 (over x), gz: 2 (over core).
Axes of the slice: x: 4, y: 2, z: 32, core: 2. Of those that a mesh axis runs over, the one named last changes fastest.
The devices are a block of a 4x8x32 slice.
Arguments:
- pair: float32 [256, 384, 384], P(('groups', 'gz'), 'gx', 'gy'), parts along dimension 0, may hold values from -6 to 6
- residue_mask: int32 [768], P('groups'), parts along dimension 0, may hold values 0 or 1
- norm_in_gain: float32 [2, 128], P(None, 'gz'), may hold values from 0.25 to 1.75
- proj_weight: bfloat16 [2, 4, 128, 128], P(None, None, None, 'gz'), may hold values from -0.5 to 0.5
- gate_weight: bfloat16 [2, 128, 128], P(None, None, 'gz'), may hold values from -0.5 to 0.5
- norm_out_gain: float32 [2, 128], P(None, 'gz'), may hold values from 0.25 to 1.75
- out_weight: bfloat16 [2, 128, 128], P(None, None, 'gz'), may hold values from -0.5 to 0.5
Outputs:
- pair_out: float32 [256, 384, 384], P(('groups', 'gz'), 'gx', 'gy'), parts along dimension 0
There are 2 independent parts, one for each index of `groups`. A program takes and returns all parts, laid end to end along the dimension named above; an argument that names none is the same for every part. Nothing has to cross between parts.
All inputs are finite; a program needn't handle non-finite values.
Results may differ from a plain program's by a relative error of at most 0.006.
Values may be sent and summed in bfloat16 or wider, within the bound.
A program may use at most 64 MiB of HBM per device.

v0:
```python
import functools

import jax
import jax.numpy as jnp
from jax import lax
from jax.experimental import pallas as pl
from jax.experimental.pallas import tpu as pltpu
from jax.sharding import PartitionSpec as P

EPSILON = 1e-05
LANES = 128
MESH = pl.DeviceIdType.MESH
F32 = jnp.float32
BF16 = jnp.bfloat16


class Geometry:
    def __init__(self, rows, cols, nz, nx):
        self.rows, self.cols, self.nz, self.nx = rows, cols, nz, nx
        self.spare = LANES - cols
        self.blocks = rows * cols // LANES
        self.extra = rows - self.blocks
        self.pieces = cols // self.spare
        self.width = self.blocks * LANES
        self.res = nz * rows
        self.near = cols // rows
        assert self.blocks * LANES == rows * cols
        assert self.extra * self.pieces == self.blocks
        assert nz * rows == nx * cols and self.near * rows == cols


def packed(geo, x):
    lead = x.shape[:-2]
    main = x[..., : geo.blocks, :]
    rest = x[..., geo.blocks :, :].reshape(*lead, geo.blocks, geo.spare)
    return jnp.concatenate([main, rest], axis=-1).reshape(*lead, geo.width)


def unpacked(geo, x):
    lead = x.shape[:-1]
    x = x.reshape(*lead, geo.blocks, LANES)
    rest = x[..., geo.cols :].reshape(*lead, geo.extra, geo.cols)
    return jnp.concatenate([x[..., : geo.cols], rest], axis=-2)


def lane_block(v, k):
    return v[:, k * LANES : (k + 1) * LANES]


def rows_of(geo, v):
    lane = lax.broadcasted_iota(jnp.int32, (v.shape[0], LANES), 1)
    rows = [jnp.where(lane < geo.cols, lane_block(v, r), 0.0) for r in range(geo.blocks)]
    for e in range(geo.extra):
        row = jnp.zeros((v.shape[0], LANES), F32)
        for q in range(geo.pieces):
            low = geo.spare * q
            piece = pltpu.roll(lane_block(v, e * geo.pieces + q), (low - geo.cols) % LANES, 1)
            row = jnp.where((lane >= low) & (lane < low + geo.spare), piece, row)
        rows.append(row)
    return rows


def block_of(geo, get_row, k):
    row = get_row(k)
    lane = lax.broadcasted_iota(jnp.int32, row.shape, 1)
    extra, q = divmod(k, geo.pieces)
    piece = pltpu.roll(get_row(geo.blocks + extra), geo.cols - geo.spare * q, 1)
    return jnp.where(lane < geo.cols, row, piece)


def normed(values, gain):
    mean = jnp.mean(values, axis=0, keepdims=True)
    centred = values - mean
    spread = jnp.mean(centred * centred, axis=0, keepdims=True)
    return (centred * lax.rsqrt(spread + EPSILON) * gain).astype(BF16)


def kernel(
    geo,
    half,
    z_ref,
    mask_ref,
    weight_ref,
    out_ref,
    z_next,
    zn,
    tmp,
    gate,
    left_out,
    right_out,
    left_all,
    right_in,
    right_all,
    left_mat,
    right_mat,
    product,
    back_out,
    back_in,
    back_other,
    triangle,
    left_sem,
    right_sem,
    right_x_sem,
    back_sem,
    other_sem,
    z_sem,
    sent_sem,
):
    nz, nx = geo.nz, geo.nx
    me_z = lax.axis_index("gx")
    me_x = lax.axis_index("gy")
    me_c = lax.axis_index("gz")
    other_c = 1 - me_c
    chunk = 3 * LANES
    chunks = [slice(k, k + chunk) for k in range(0, geo.width, chunk)]

    barrier = pltpu.get_barrier_semaphore()

    def signal_z(k, _):
        pl.semaphore_signal(
            barrier, inc=1, device_id={"gx": lax.rem(me_z + 1 + k, nz)}, device_id_type=MESH
        )
        return _

    lax.fori_loop(0, nz - 1, signal_z, 0)
    for k in range(1, nx):
        pl.semaphore_signal(
            barrier, inc=1, device_id={"gy": lax.rem(me_x + k, nx)}, device_id_type=MESH
        )
    pl.semaphore_signal(barrier, inc=1, device_id={"gz": other_c}, device_id_type=MESH)

    def far_first(k):
        m = (k + 1) // 2
        return lax.rem(me_z + nz // 2 + m * (1 - 2 * (k % 2)), nz)

    def copy_z(src, dst, send, recv, to):
        return pltpu.make_async_remote_copy(
            src_ref=src, dst_ref=dst, send_sem=send, recv_sem=recv, device_id={"gx": to}, device_id_type=MESH
        )

    def copy_x(src, dst, send, recv, to):
        return pltpu.make_async_remote_copy(
            src_ref=src, dst_ref=dst, send_sem=send, recv_sem=recv, device_id={"gy": to}, device_id_type=MESH
        )

    def copy_c(src, dst, send, recv):
        return pltpu.make_async_remote_copy(
            src_ref=src, dst_ref=dst, send_sem=send, recv_sem=recv, device_id={"gz": other_c}, device_id_type=MESH
        )

    def store_rows(mat, lead, base, value):
        for r, row in enumerate(rows_of(geo, value)):
            for h in range(2):
                mat[lead, h, pl.ds(base + r, 1), :] = row[h : h + 1, :]

    for u in range(2):
        weights = weight_ref.at[u]
        left_u, right_u = left_out.at[u], right_out.at[u]

        if u == 1:
            copy_c(z_next.at[me_c], z_next.at[me_c], sent_sem.at[5, 0], z_sem).wait_recv()
        gain_in = z_ref[:, geo.width + u : geo.width + u + 1]
        for s in chunks:
            if u == 0:
                z = z_ref[:, s]
            else:
                z = jnp.concatenate([z_next[0, :, s], z_next[1, :, s]], axis=0)
            zn[:, s] = normed(z, gain_in)

        def project(first):
            for s in chunks:
                both = jnp.dot(
                    weights[first : first + 2 * half, :], zn[:, s], preferred_element_type=F32
                )
                tmp[:, s] = jax.nn.sigmoid(both[:half]) * both[half:] * mask_ref[:, s]

        def to_messages(out):
            for k in range(nz):
                out[k] = tmp[2 * k : 2 * k + 2, :].astype(BF16)

        project(0)
        to_messages(left_u)
        if u == 0:
            pl.semaphore_wait(barrier, nz - 1 + nx - 1 + 1)

        def send_left(k, _):
            to = far_first(k)
            copy_z(
                left_u.at[to],
                left_all.at[u, me_x, me_z],
                sent_sem.at[0, u],
                left_sem.at[u, me_x, me_z],
                to,
            ).start()
            return _

        lax.fori_loop(0, nz - 1, send_left, 0)

        def forward_left(src, s):
            for k in range(1, nx):
                copy_x(
                    src,
                    left_all.at[u, me_x, s],
                    sent_sem.at[2, u],
                    left_sem.at[u, me_x, s],
                    lax.rem(me_x + k, nx),
                ).start()

        forward_left(left_u.at[me_z], me_z)

        project(2 * half)
        to_messages(right_u)

        def send_right(k, _):
            to = far_first(k)
            copy_z(
                right_u.at[to],
                right_in.at[u, me_z],
                sent_sem.at[1, u],
                right_sem.at[u, me_z],
                to,
            ).start()
            return _

        lax.fori_loop(0, nz - 1, send_right, 0)

        def forward_right(src, s):
            target = s // geo.near

            @pl.when(target != me_x)
            def run():
                copy_x(
                    src,
                    right_all.at[me_x, s % geo.near],
                    sent_sem.at[3, 0],
                    right_x_sem.at[me_x, s % geo.near],
                    target,
                ).start()

        if u == 0:
            forward_right(right_u.at[me_z], me_z)

        for s in chunks:
            gate[:, s] = jax.nn.sigmoid(
                jnp.dot(weights[4 * half : 5 * half, :], zn[:, s], preferred_element_type=F32)
            )

        store_rows(left_mat, me_x, me_z * geo.rows, left_u[me_z].astype(F32))

        def take_left(k, _):
            s = far_first(k)
            slot = left_all.at[u, me_x, s]
            copy_z(slot, slot, sent_sem.at[0, u], left_sem.at[u, me_x, s], s).wait_recv()
            forward_left(slot, s)
            store_rows(left_mat, me_x, s * geo.rows, left_all[u, me_x, s].astype(F32))
            return _

        lax.fori_loop(0, nz - 1, take_left, 0)

        if u == 0:
            @pl.when(me_z // geo.near == me_x)
            def run():
                store_rows(
                    right_mat, me_x, (me_z % geo.near) * geo.rows, right_u[me_z].astype(F32)
                )
        else:
            store_rows(right_mat, 0, me_z * geo.rows, right_u[me_z].astype(F32))

        def take_right(k, _):
            s = far_first(k)
            slot = right_in.at[u, s]
            copy_z(slot, slot, sent_sem.at[1, u], right_sem.at[u, s], s).wait_recv()
            if u == 0:
                forward_right(slot, s)

                @pl.when(s // geo.near == me_x)
                def run():
                    store_rows(
                        right_mat, me_x, (s % geo.near) * geo.rows, right_in[u, s].astype(F32)
                    )
            else:
                store_rows(right_mat, 0, s * geo.rows, right_in[u, s].astype(F32))
            return _

        lax.fori_loop(0, nz - 1, take_right, 0)

        for d in range(1, nx):
            x = lax.rem(me_x + d, nx)

            def take_left_x(k, _):
                slot = left_all.at[u, x, k]
                copy_x(slot, slot, sent_sem.at[2, u], left_sem.at[u, x, k], x).wait_recv()
                store_rows(left_mat, x, k * geo.rows, left_all[u, x, k].astype(F32))
                return _

            lax.fori_loop(0, nz, take_left_x, 0)

            if u == 0:

                def take_right_x(k, _):
                    slot = right_all.at[x, k]
                    copy_x(slot, slot, sent_sem.at[3, 0], right_x_sem.at[x, k], x).wait_recv()
                    store_rows(right_mat, x, k * geo.rows, right_all[x, k].astype(F32))
                    return _

                lax.fori_loop(0, geo.near, take_right_x, 0)

        for h in range(2):
            if u == 0:
                total = jnp.zeros((geo.res, geo.cols), F32)
                for x in range(nx):
                    total += lax.dot_general(
                        left_mat[x, h].astype(BF16),
                        right_mat[x, h, : geo.cols, :].astype(BF16),
                        (((1,), (1,)), ((), ())),
                        preferred_element_type=F32,
                    )
                product[h, :, : geo.cols] = total
            else:
                right = right_mat[0, h].astype(BF16)
                for x in range(nx):
                    part = lax.dot_general(
                        left_mat[x, h].astype(BF16),
                        right,
                        (((0,), (0,)), ((), ())),
                        preferred_element_type=F32,
                    )
                    product[h, geo.cols * x : geo.cols * (x + 1), :] = part[: geo.cols, :]

        back_u = back_out.at[u]

        def block_row(base, r):
            return jnp.concatenate([product[h, pl.ds(base + r, 1), :] for h in range(2)], axis=0)

        def build_back(to):
            base = to * geo.rows
            for k in range(geo.blocks):
                value = block_of(geo, functools.partial(block_row, base), k)
                back_u[to, :, k * LANES : (k + 1) * LANES] = value.astype(BF16)

        def send_back(k, _):
            to = far_first(k)
            build_back(to)
            copy_z(
                back_u.at[to], back_in.at[u, me_z], sent_sem.at[4, u], back_sem.at[u, me_z], to
            ).start()
            return _

        lax.fori_loop(0, nz - 1, send_back, 0)
        build_back(me_z)

        def forward_back(src, s):
            copy_c(src, back_other.at[u, s], sent_sem.at[6, u], other_sem.at[u, s]).start()

        forward_back(back_u.at[me_z], me_z)
        triangle[me_c, me_z] = back_u[me_z].astype(F32)

        def take_back(k, _):
            s = far_first(k)
            slot = back_in.at[u, s]
            copy_z(slot, slot, sent_sem.at[4, u], back_sem.at[u, s], s).wait_recv()
            forward_back(slot, s)
            triangle[me_c, s] = back_in[u, s].astype(F32)
            return _

        lax.fori_loop(0, nz - 1, take_back, 0)

        def take_other(k, _):
            slot = back_other.at[u, k]
            copy_c(slot, slot, sent_sem.at[6, u], other_sem.at[u, k]).wait_recv()
            triangle[other_c, k] = back_other[u, k].astype(F32)
            return _

        lax.fori_loop(0, nz, take_other, 0)

        gain_out = z_ref[:, geo.width + 2 + u : geo.width + 3 + u]
        for s in chunks:
            values = jnp.concatenate(
                [triangle[c, k, :, s] for c in range(2) for k in range(nz)], axis=0
            )
            tn = normed(values, gain_out)
            change = jnp.dot(weights[5 * half :, :], tn, preferred_element_type=F32)
            if u == 0:
                mine = z_ref[pl.ds(pl.multiple_of(me_c * half, half), half), s]
                z_next[me_c, :, s] = mine + gate[:, s] * change
            else:
                out_ref[:, s] = z_next[me_c, :, s] + gate[:, s] * change
        if u == 0:
            copy_c(z_next.at[me_c], z_next.at[me_c], sent_sem.at[5, 0], z_sem).start()

    for u in range(2):
        many = left_out.at[u, pl.ds(0, nz - 1)]
        copy_z(many, many, sent_sem.at[0, u], z_sem, me_z).wait_send()
        copy_z(many, many, sent_sem.at[1, u], z_sem, me_z).wait_send()
        copy_z(many, many, sent_sem.at[4, u], z_sem, me_z).wait_send()
        for k in range(1, nx):
            all_slots = left_out.at[u]
            copy_x(all_slots, all_slots, sent_sem.at[2, u], z_sem, me_x).wait_send()
        every = left_out.at[u]
        copy_c(every, every, sent_sem.at[6, u], z_sem).wait_send()
    away = left_out.at[0, pl.ds(0, nz - geo.near)]
    copy_x(away, away, sent_sem.at[3, 0], z_sem, me_x).wait_send()
    copy_c(z_next.at[me_c], z_next.at[me_c], sent_sem.at[5, 0], z_sem).wait_send()


def per_device(
    geo, pair, residue_mask, norm_in_gain, proj_weight, gate_weight, norm_out_gain, out_weight
):
    half = pair.shape[0]
    full = 2 * half
    row_start = lax.axis_index("gx") * geo.rows
    col_start = lax.axis_index("gy") * geo.cols
    row_flags = lax.dynamic_slice_in_dim(residue_mask, row_start, geo.rows).astype(F32)
    col_flags = lax.dynamic_slice_in_dim(residue_mask, col_start, geo.cols).astype(F32)
    mask = packed(geo, row_flags[:, None] * col_flags[None, :])[None, :]
    gains = jnp.concatenate([norm_in_gain, norm_out_gain], axis=0).T
    gains = jnp.pad(gains, ((0, 0), (0, LANES - 4)))
    z = jnp.concatenate([packed(geo, pair), gains], axis=1)
    z = lax.all_gather(z, "gz", axis=0, tiled=True)
    weights = jnp.concatenate(
        [proj_weight, gate_weight[:, None], out_weight[:, None]], axis=1
    )
    weights = jnp.swapaxes(weights, 2, 3).reshape(2, 6 * half, full)

    nz, nx = geo.nz, geo.nx
    vmem = pltpu.VMEM
    message = (2, geo.width)
    dma = pltpu.SemaphoreType.DMA
    result = pl.pallas_call(
        functools.partial(kernel, geo, half),
        out_shape=jax.ShapeDtypeStruct((half, geo.width), F32),
        in_specs=[pl.BlockSpec(memory_space=vmem)] * 3,
        out_specs=pl.BlockSpec(memory_space=vmem),
        scratch_shapes=[
            vmem((2, half, geo.width), F32),
            vmem((full, geo.width), BF16),
            vmem((half, geo.width), F32),
            vmem((half, geo.width), F32),
            vmem((2, nz, *message), BF16),
            vmem((2, nz, *message), BF16),
            vmem((2, nx, nz, *message), BF16),
            vmem((2, nz, *message), BF16),
            vmem((nx, geo.near, *message), BF16),
            vmem((nx, 2, geo.res, LANES), F32),
            vmem((nx, 2, geo.res, LANES), F32),
            vmem((2, geo.res, LANES), F32),
            vmem((2, nz, *message), BF16),
            vmem((2, nz, *message), BF16),
            vmem((2, nz, *message), BF16),
            vmem((2, nz, *message), F32),
            dma((2, nx, nz)),
            dma((2, nz)),
            dma((nx, geo.near)),
            dma((2, nz)),
            dma((2, nz)),
            dma,
            dma((7, 2)),
        ],
        compiler_params=pltpu.CompilerParams(
            collective_id=0, has_side_effects=True, vmem_limit_bytes=60 * 1024 * 1024
        ),
        name="triangle_updates",
    )(z, mask, weights)
    return unpacked(geo, result)


def solution(mesh):
    def body(pair, *rest):
        geo = Geometry(pair.shape[1], pair.shape[2], mesh.shape["gx"], mesh.shape["gy"])
        return per_device(geo, pair, *rest)

    return jax.shard_map(
        body,
        mesh=mesh,
        in_specs=(
            P(("groups", "gz"), "gx", "gy"),
            P("groups"),
            P(None, "gz"),
            P(None, None, None, "gz"),
            P(None, None, "gz"),
            P(None, "gz"),
            P(None, None, "gz"),
        ),
        out_specs=P(("groups", "gz"), "gx", "gy"),
        check_vma=False,
    )
```

profile of v0, /device:TPU:33, one launch (start us, length us, event | category | flops | bytes accessed | tf_op | source)
XLA Modules:
  0.0 188.7 jit_solution(3543148647577586710)
XLA Ops:
  0.0 0.0 copy-start.5
  0.0 0.7 copy-done.5
  0.7 0.1 dynamic-slice_convert_fusion
  0.8 0.1 dynamic-slice_convert_fusion.1
  0.8 0.0 copy-start.4
  0.8 0.7 copy-done.4
  1.5 0.0 copy-done.3
  1.5 0.1 broadcast_multiply_fusion
  1.6 0.1 reshape.22
  1.7 0.1 maximum_bitcast_fusion.1
  1.8 0.6 copy.38
  2.4 0.1 copy.27
  2.5 0.9 slice-done
  3.4 0.1 copy.33
  3.5 0.0 copy-start
  3.5 0.0 copy-start.1
  3.5 0.0 copy-start.2
  3.5 0.2 copy.25
  3.7 0.7 copy-done
  4.4 0.0 copy-done.1
  4.4 0.0 copy-done.2
  4.4 0.7 pad_maximum_fusion.1
  5.1 1.0 slice-done.1
  6.1 0.1 copy_bitcast_fusion
  6.2 43.5 %all_gather.3.z_ref = f32[128,1280]{1,0:T(8,128)} all-gather(f32[64,1280]{1,0:T(8,128)S(1)} %select_maximum_fusion), channel_id=1, replica_groups=mesh['groups'=2,'gx'=32,'gy'=4,'gz'=2] {'gz'}, dimensions={0}, use_global_device_ids=true | all-gather | bytes 983040 | tf_op jit(solution)/shard_map/all_gather | solution.py:419
  49.8 136.4 %triangle_updates.1 = f32[64,1152]{1,0:T(8,128)} custom-call(f32[128,1280]{1,0:T(8,128)} %all_gather.3.z_ref, f32[1,1152]{1,0:T(1,128)} %bitcast.33, bf16[2,384,128]{2,1,0:T(8,128)(2,1)} %bitcast.26), custom_call_target="tpu_custom_call" | custom-call | tf_op jit(solution)/shard_map/triangle_updates/pallas_call | solution.py:429
  186.2 1.0 reshape.24
  187.2 0.2 slice.27
  187.4 0.2 copy.30
  187.6 0.1 copy.31
  187.7 0.1 pad_maximum_fusion
  187.8 0.9 copy.32
  (6 shorter events, 0.0 us)
Async XLA Ops:
  0.0 0.7 copy-start.5
  0.8 0.7 copy-start.4
  0.8 0.7 copy-start.3
  2.5 0.9 slice-start
  3.5 0.9 copy-start
  3.5 0.9 copy-start.1
  3.5 0.9 copy-start.2
  5.1 1.0 slice-start.1
where the time goes:
time: 189 us
  Pallas kernels  136 us (72%)
  blocking collectives  43.5 us (23%)
  local copies, waits for them, and re-layouts  7.38 us (4%)
    pallas_call x1, Pallas kernels, per_device(): pl.pallas_call(functools.partial(kernel, geo, half), out_shape=jax.ShapeD...  136 us
    all_gather x1, blocking collectives, per_device(): z = lax.all_gather(z, 'gz', axis=0, tiled=True)  43.5 us

commit v1 on v0

--- a/solution.py
+++ b/solution.py
@@ -34,13 +34,6 @@
     main = x[..., : geo.blocks, :]
     rest = x[..., geo.blocks :, :].reshape(*lead, geo.blocks, geo.spare)
     return jnp.concatenate([main, rest], axis=-1).reshape(*lead, geo.width)
-
-
-def unpacked(geo, x):
-    lead = x.shape[:-1]
-    x = x.reshape(*lead, geo.blocks, LANES)
-    rest = x[..., geo.cols :].reshape(*lead, geo.extra, geo.cols)
-    return jnp.concatenate([x[..., : geo.cols], rest], axis=-2)
 
 
 def lane_block(v, k):
@@ -111,7 +104,7 @@
     me_x = lax.axis_index("gy")
     me_c = lax.axis_index("gz")
     other_c = 1 - me_c
-    chunk = 3 * LANES
+    chunk = geo.pieces * LANES
     chunks = [slice(k, k + chunk) for k in range(0, geo.width, chunk)]
 
     barrier = pltpu.get_barrier_semaphore()
@@ -153,48 +146,31 @@
             for h in range(2):
                 mat[lead, h, pl.ds(base + r, 1), :] = row[h : h + 1, :]
 
+    group = 4
+    lag = 8
+
     for u in range(2):
         weights = weight_ref.at[u]
-        left_u, right_u = left_out.at[u], right_out.at[u]
-
-        if u == 1:
-            copy_c(z_next.at[me_c], z_next.at[me_c], sent_sem.at[5, 0], z_sem).wait_recv()
+        left_u, right_u, back_u = left_out.at[u], right_out.at[u], back_out.at[u]
+
         gain_in = z_ref[:, geo.width + u : geo.width + u + 1]
-        for s in chunks:
+        for i, s in enumerate(chunks):
             if u == 0:
                 z = z_ref[:, s]
             else:
+                piece = z_next.at[me_c, :, s]
+                copy_c(piece, piece, sent_sem.at[5, 0], z_sem.at[i]).wait_recv()
                 z = jnp.concatenate([z_next[0, :, s], z_next[1, :, s]], axis=0)
             zn[:, s] = normed(z, gain_in)
 
-        def project(first):
+        def project(first, out):
             for s in chunks:
                 both = jnp.dot(
                     weights[first : first + 2 * half, :], zn[:, s], preferred_element_type=F32
                 )
                 tmp[:, s] = jax.nn.sigmoid(both[:half]) * both[half:] * mask_ref[:, s]
-
-        def to_messages(out):
             for k in range(nz):
                 out[k] = tmp[2 * k : 2 * k + 2, :].astype(BF16)
-
-        project(0)
-        to_messages(left_u)
-        if u == 0:
-            pl.semaphore_wait(barrier, nz - 1 + nx - 1 + 1)
-
-        def send_left(k, _):
-            to = far_first(k)
-            copy_z(
-                left_u.at[to],
-                left_all.at[u, me_x, me_z],
-                sent_sem.at[0, u],
-                left_sem.at[u, me_x, me_z],
-                to,
-            ).start()
-            return _
-
-        lax.fori_loop(0, nz - 1, send_left, 0)
 
         def forward_left(src, s):
             for k in range(1, nx):
@@ -206,24 +182,6 @@
                     lax.rem(me_x + k, nx),
                 ).start()
 
-        forward_left(left_u.at[me_z], me_z)
-
-        project(2 * half)
-        to_messages(right_u)
-
-        def send_right(k, _):
-            to = far_first(k)
-            copy_z(
-                right_u.at[to],
-                right_in.at[u, me_z],
-                sent_sem.at[1, u],
-                right_sem.at[u, me_z],
-                to,
-            ).start()
-            return _
-
-        lax.fori_loop(0, nz - 1, send_right, 0)
-
         def forward_right(src, s):
             target = s // geo.near
 
@@ -237,65 +195,126 @@
                     target,
                 ).start()
 
-        if u == 0:
-            forward_right(right_u.at[me_z], me_z)
-
-        for s in chunks:
-            gate[:, s] = jax.nn.sigmoid(
-                jnp.dot(weights[4 * half : 5 * half, :], zn[:, s], preferred_element_type=F32)
-            )
-
-        store_rows(left_mat, me_x, me_z * geo.rows, left_u[me_z].astype(F32))
-
-        def take_left(k, _):
+        def send_left():
+            def send(k, _):
+                to = far_first(k)
+                copy_z(
+                    left_u.at[to],
+                    left_all.at[u, me_x, me_z],
+                    sent_sem.at[0, u],
+                    left_sem.at[u, me_x, me_z],
+                    to,
+                ).start()
+                return _
+
+            lax.fori_loop(0, nz - 1, send, 0)
+            forward_left(left_u.at[me_z], me_z)
+            left_all[u, me_x, me_z] = left_u[me_z]
+
+        def send_right():
+            def send(k, _):
+                to = far_first(k)
+                copy_z(
+                    right_u.at[to],
+                    right_in.at[u, me_z],
+                    sent_sem.at[1, u],
+                    right_sem.at[u, me_z],
+                    to,
+                ).start()
+                return _
+
+            lax.fori_loop(0, nz - 1, send, 0)
+            right_in[u, me_z] = right_u[me_z]
+
+        def open_gate():
+            for s in chunks:
+                gate[:, s] = jax.nn.sigmoid(
+                    jnp.dot(weights[4 * half : 5 * half, :], zn[:, s], preferred_element_type=F32)
+                )
+
+        def left_base(k, s):
+            return (k if u == 0 else s) * geo.rows
+
+        def take_left(k):
             s = far_first(k)
             slot = left_all.at[u, me_x, s]
-            copy_z(slot, slot, sent_sem.at[0, u], left_sem.at[u, me_x, s], s).wait_recv()
-            forward_left(slot, s)
-            store_rows(left_mat, me_x, s * geo.rows, left_all[u, me_x, s].astype(F32))
-            return _
-
-        lax.fori_loop(0, nz - 1, take_left, 0)
+
+            @pl.when(k < nz - 1)
+            def run():
+                copy_z(slot, slot, sent_sem.at[0, u], left_sem.at[u, me_x, s], s).wait_recv()
+                forward_left(slot, s)
+
+            store_rows(left_mat, me_x, left_base(k, s), left_all[u, me_x, s].astype(F32))
+
+        def take_left_x(k):
+            s = far_first(k)
+            for d in range(1, nx):
+                x = lax.rem(me_x + d, nx)
+                slot = left_all.at[u, x, s]
+                copy_x(slot, slot, sent_sem.at[2, u], left_sem.at[u, x, s], x).wait_recv()
+                store_rows(left_mat, x, left_base(k, s), left_all[u, x, s].astype(F32))
+
+        def wait_right(k, s):
+            slot = right_in.at[u, s]
+
+            @pl.when(k < nz - 1)
+            def run():
+                copy_z(slot, slot, sent_sem.at[1, u], right_sem.at[u, s], s).wait_recv()
+
+        def block_row(base, r):
+            return jnp.concatenate([product[h, pl.ds(base + r, 1), :] for h in range(2)], axis=0)
+
+        def send_back(k):
+            to = far_first(k)
+            base = left_base(k, to)
+            for b in range(geo.blocks):
+                value = block_of(geo, functools.partial(block_row, base), b)
+                back_u[to, :, b * LANES : (b + 1) * LANES] = value.astype(BF16)
+
+            @pl.when(k < nz - 1)
+            def run():
+                copy_z(
+                    back_u.at[to], back_in.at[u, me_z], sent_sem.at[4, u], back_sem.at[u, me_z], to
+                ).start()
 
         if u == 0:
-            @pl.when(me_z // geo.near == me_x)
-            def run():
-                store_rows(
-                    right_mat, me_x, (me_z % geo.near) * geo.rows, right_u[me_z].astype(F32)
-                )
-        else:
-            store_rows(right_mat, 0, me_z * geo.rows, right_u[me_z].astype(F32))
-
-        def take_right(k, _):
-            s = far_first(k)
-            slot = right_in.at[u, s]
-            copy_z(slot, slot, sent_sem.at[1, u], right_sem.at[u, s], s).wait_recv()
-            if u == 0:
-                forward_right(slot, s)
+            project(2 * half, right_u)
+            pl.semaphore_wait(barrier, nz - 1 + nx - 1 + 1)
+            send_right()
+            forward_right(right_u.at[me_z], me_z)
+            project(0, left_u)
+            send_left()
+            open_gate()
+
+            def take_right(k, _):
+                s = far_first(k)
+                wait_right(k, s)
+
+                @pl.when(k < nz - 1)
+                def run():
+                    forward_right(right_in.at[0, s], s)
 
                 @pl.when(s // geo.near == me_x)
-                def run():
+                def run_own():
                     store_rows(
-                        right_mat, me_x, (s % geo.near) * geo.rows, right_in[u, s].astype(F32)
+                        right_mat, me_x, (s % geo.near) * geo.rows, right_in[0, s].astype(F32)
                     )
-            else:
-                store_rows(right_mat, 0, s * geo.rows, right_in[u, s].astype(F32))
-            return _
-
-        lax.fori_loop(0, nz - 1, take_right, 0)
-
-        for d in range(1, nx):
-            x = lax.rem(me_x + d, nx)
-
-            def take_left_x(k, _):
-                slot = left_all.at[u, x, k]
-                copy_x(slot, slot, sent_sem.at[2, u], left_sem.at[u, x, k], x).wait_recv()
-                store_rows(left_mat, x, k * geo.rows, left_all[u, x, k].astype(F32))
-                return _
-
-            lax.fori_loop(0, nz, take_left_x, 0)
-
-            if u == 0:
+
+                return _
+
+            lax.fori_loop(0, nz, take_right, 0)
+
+            def take_group(g):
+                def take(i, _):
+                    take_left(g * group + i)
+                    return _
+
+                lax.fori_loop(0, group, take, 0)
+
+            take_group(0)
+
+            for d in range(1, nx):
+                x = lax.rem(me_x + d, nx)
 
                 def take_right_x(k, _):
                     slot = right_all.at[x, k]
@@ -304,19 +323,72 @@
                     return _
 
                 lax.fori_loop(0, geo.near, take_right_x, 0)
-
-        for h in range(2):
-            if u == 0:
-                total = jnp.zeros((geo.res, geo.cols), F32)
-                for x in range(nx):
-                    total += lax.dot_general(
-                        left_mat[x, h].astype(BF16),
-                        right_mat[x, h, : geo.cols, :].astype(BF16),
-                        (((1,), (1,)), ((), ())),
-                        preferred_element_type=F32,
-                    )
-                product[h, :, : geo.cols] = total
-            else:
+            take_group(1)
+
+            tall = group * geo.rows
+
+            def work(g, _):
+                @pl.when(g < nz // group - 2)
+                def run():
+                    take_group(g + 2)
+
+                def take_x(i, _):
+                    take_left_x(g * group + i)
+                    return _
+
+                lax.fori_loop(0, group, take_x, 0)
+                rows = pl.ds(pl.multiple_of(g * tall, tall), tall)
+                for h in range(2):
+                    total = jnp.zeros((tall, geo.cols), F32)
+                    for x in range(nx):
+                        total += lax.dot_general(
+                            left_mat[x, h, rows, :].astype(BF16),
+                            right_mat[x, h, : geo.cols, :].astype(BF16),
+                            (((1,), (1,)), ((), ())),
+                            preferred_element_type=F32,
+                        )
+                    product[h, rows, : geo.cols] = total
+
+                def send(i, _):
+                    send_back(g * group + i)
+                    return _
+
+                lax.fori_loop(0, group, send, 0)
+                return _
+
+            lax.fori_loop(0, nz // group, work, 0)
+        else:
+            project(0, left_u)
+            send_left()
+            project(2 * half, right_u)
+            send_right()
+            open_gate()
+
+            def take_lefts(k, _):
+                take_left(k)
+
+                @pl.when(k >= lag)
+                def run():
+                    take_left_x(k - lag)
+
+                return _
+
+            lax.fori_loop(0, nz, take_lefts, 0)
+
+            def take_right(k, _):
+                s = far_first(k)
+                wait_right(k, s)
+                store_rows(right_mat, 0, s * geo.rows, right_in[1, s].astype(F32))
+
+                @pl.when(k < lag)
+                def run():
+                    take_left_x(nz - lag + k)
+
+                return _
+
+            lax.fori_loop(0, nz, take_right, 0)
+
+            for h in range(2):
                 right = right_mat[0, h].astype(BF16)
                 for x in range(nx):
                     part = lax.dot_general(
@@ -327,42 +399,24 @@
                     )
                     product[h, geo.cols * x : geo.cols * (x + 1), :] = part[: geo.cols, :]
 
-        back_u = back_out.at[u]
-
-        def block_row(base, r):
-            return jnp.concatenate([product[h, pl.ds(base + r, 1), :] for h in range(2)], axis=0)
-
-        def build_back(to):
-            base = to * geo.rows
-            for k in range(geo.blocks):
-                value = block_of(geo, functools.partial(block_row, base), k)
-                back_u[to, :, k * LANES : (k + 1) * LANES] = value.astype(BF16)
-
-        def send_back(k, _):
-            to = far_first(k)
-            build_back(to)
-            copy_z(
-                back_u.at[to], back_in.at[u, me_z], sent_sem.at[4, u], back_sem.at[u, me_z], to
-            ).start()
-            return _
-
-        lax.fori_loop(0, nz - 1, send_back, 0)
-        build_back(me_z)
-
-        def forward_back(src, s):
-            copy_c(src, back_other.at[u, s], sent_sem.at[6, u], other_sem.at[u, s]).start()
-
-        forward_back(back_u.at[me_z], me_z)
-        triangle[me_c, me_z] = back_u[me_z].astype(F32)
+            def send(k, _):
+                send_back(k)
+                return _
+
+            lax.fori_loop(0, nz, send, 0)
 
         def take_back(k, _):
             s = far_first(k)
             slot = back_in.at[u, s]
             copy_z(slot, slot, sent_sem.at[4, u], back_sem.at[u, s], s).wait_recv()
-            forward_back(slot, s)
+            copy_c(slot, back_other.at[u, s], sent_sem.at[6, u], other_sem.at[u, s]).start()
             triangle[me_c, s] = back_in[u, s].astype(F32)
             return _
 
+        copy_c(
+            back_u.at[me_z], back_other.at[u, me_z], sent_sem.at[6, u], other_sem.at[u, me_z]
+        ).start()
+        triangle[me_c, me_z] = back_u[me_z].astype(F32)
         lax.fori_loop(0, nz - 1, take_back, 0)
 
         def take_other(k, _):
@@ -374,7 +428,7 @@
         lax.fori_loop(0, nz, take_other, 0)
 
         gain_out = z_ref[:, geo.width + 2 + u : geo.width + 3 + u]
-        for s in chunks:
+        for i, s in enumerate(chunks):
             values = jnp.concatenate(
                 [triangle[c, k, :, s] for c in range(2) for k in range(nz)], axis=0
             )
@@ -383,24 +437,34 @@
             if u == 0:
                 mine = z_ref[pl.ds(pl.multiple_of(me_c * half, half), half), s]
                 z_next[me_c, :, s] = mine + gate[:, s] * change
+                piece = z_next.at[me_c, :, s]
+                copy_c(piece, piece, sent_sem.at[5, 0], z_sem.at[i]).start()
             else:
-                out_ref[:, s] = z_next[me_c, :, s] + gate[:, s] * change
-        if u == 0:
-            copy_c(z_next.at[me_c], z_next.at[me_c], sent_sem.at[5, 0], z_sem).start()
-
+                value = z_next[me_c, :, s] + gate[:, s] * change
+                lane = lax.broadcasted_iota(jnp.int32, (half, LANES), 1)
+                row = jnp.zeros((half, LANES), F32)
+                for q in range(geo.pieces):
+                    block = lane_block(value, q)
+                    out_ref[:, i * geo.pieces + q, :] = block[:, : geo.cols]
+                    low = geo.spare * q
+                    moved = pltpu.roll(block, (low - geo.cols) % LANES, 1)
+                    row = jnp.where((lane >= low) & (lane < low + geo.spare), moved, row)
+                out_ref[:, geo.blocks + i, :] = row[:, : geo.cols]
+
+    any_sem = z_sem.at[0]
     for u in range(2):
         many = left_out.at[u, pl.ds(0, nz - 1)]
-        copy_z(many, many, sent_sem.at[0, u], z_sem, me_z).wait_send()
-        copy_z(many, many, sent_sem.at[1, u], z_sem, me_z).wait_send()
-        copy_z(many, many, sent_sem.at[4, u], z_sem, me_z).wait_send()
+        copy_z(many, many, sent_sem.at[0, u], any_sem, me_z).wait_send()
+        copy_z(many, many, sent_sem.at[1, u], any_sem, me_z).wait_send()
+        copy_z(many, many, sent_sem.at[4, u], any_sem, me_z).wait_send()
         for k in range(1, nx):
             all_slots = left_out.at[u]
-            copy_x(all_slots, all_slots, sent_sem.at[2, u], z_sem, me_x).wait_send()
+            copy_x(all_slots, all_slots, sent_sem.at[2, u], any_sem, me_x).wait_send()
         every = left_out.at[u]
-        copy_c(every, every, sent_sem.at[6, u], z_sem).wait_send()
+        copy_c(every, every, sent_sem.at[6, u], any_sem).wait_send()
     away = left_out.at[0, pl.ds(0, nz - geo.near)]
-    copy_x(away, away, sent_sem.at[3, 0], z_sem, me_x).wait_send()
-    copy_c(z_next.at[me_c], z_next.at[me_c], sent_sem.at[5, 0], z_sem).wait_send()
+    copy_x(away, away, sent_sem.at[3, 0], any_sem, me_x).wait_send()
+    copy_c(z_next.at[me_c], z_next.at[me_c], sent_sem.at[5, 0], any_sem).wait_send()
 
 
 def per_device(
@@ -426,9 +490,9 @@
     vmem = pltpu.VMEM
     message = (2, geo.width)
     dma = pltpu.SemaphoreType.DMA
-    result = pl.pallas_call(
+    return pl.pallas_call(
         functools.partial(kernel, geo, half),
-        out_shape=jax.ShapeDtypeStruct((half, geo.width), F32),
+        out_shape=jax.ShapeDtypeStruct(pair.shape, F32),
         in_specs=[pl.BlockSpec(memory_space=vmem)] * 3,
         out_specs=pl.BlockSpec(memory_space=vmem),
         scratch_shapes=[
@@ -453,7 +517,7 @@
             dma((nx, geo.near)),
             dma((2, nz)),
             dma((2, nz)),
-            dma,
+            dma((geo.extra,)),
             dma((7, 2)),
         ],
         compiler_params=pltpu.CompilerParams(
@@ -461,7 +525,6 @@
         ),
         name="triangle_updates",
     )(z, mask, weights)
-    return unpacked(geo, result)
 
 
 def solution(mesh):

time: 189 us -> 174 us (0.921)
  Pallas kernels: 136 us -> 122 us
    pallas_call x1, Pallas kernels: 136 us -> 122 us  [per_device(): pl.pallas_call(functools.partial(kernel, geo, half), out_shape=jax.ShapeD...]
    pallas_call x0 -> x1, local copies, waits for them, and re-layouts: none -> 1.92 us  [per_device(): pl.pallas_call(functools.partial(kernel, geo, half), out_shape=jax.ShapeD...]
where the time goes in v1:
time: 174 us; the launch traced here: 173 us
  Pallas kernels  122 us (70%)
  blocking collectives  43.5 us (25%)
  local copies, waits for them, and re-layouts  6.92 us (4%)
    pallas_call x1, Pallas kernels, per_device(): pl.pallas_call(functools.partial(kernel, geo, half), out_shape=jax.ShapeD...  122 us
    all_gather x1, blocking collectives, per_device(): z = lax.all_gather(z, 'gz', axis=0, tiled=True)  43.5 us

profile of v1, /device:TPU:33, one launch (start us, length us, event | category | flops | bytes accessed | tf_op | source)
XLA Modules:
  0.0 173.4 jit_solution(16630434685903725575)
XLA Ops:
  0.0 0.0 copy-start.5
  0.0 0.7 copy-done.5
  0.7 0.1 dynamic-slice_convert_fusion
  0.8 0.1 dynamic-slice_convert_fusion.1
  0.8 0.0 copy-start.4
  0.8 0.0 copy-start.3
  0.8 0.7 copy-done.4
  1.5 0.0 copy-done.3
  1.5 0.1 broadcast_multiply_fusion
  1.6 0.1 reshape.16
  1.7 0.1 maximum_bitcast_fusion.1
  1.8 0.6 copy.34
  2.4 0.1 copy.25
  2.5 0.0 slice-start
  2.5 0.9 slice-done
  3.4 0.1 copy.29
  3.5 0.0 copy-start
  3.5 0.0 copy-start.1
  3.5 0.0 copy-start.2
  3.5 0.2 copy.23
  3.7 0.7 copy-done
  4.4 0.0 copy-done.1
  4.4 0.0 copy-done.2
  4.4 0.7 pad_maximum_fusion
  5.1 0.0 slice-start.1
  5.1 1.0 slice-done.1
  6.0 0.1 copy_bitcast_fusion
  6.2 43.5 %all_gather.3.z_ref = f32[128,1280]{1,0:T(8,128)} all-gather(f32[64,1280]{1,0:T(8,128)S(1)} %select_maximum_fusion), channel_id=1, replica_groups=mesh['groups'=2,'gx'=32,'gy'=4,'gz'=2] {'gz'}, dimensions={0}, use_global_device_ids=true | all-gather | bytes 983040 | tf_op jit(solution)/shard_map/all_gather | solution.py:483
  49.7 121.8 %triangle_updates.1 = f32[64,12,96]{2,1,0:T(8,128)} custom-call(f32[128,1280]{1,0:T(8,128)} %all_gather.3.z_ref, f32[1,1152]{1,0:T(1,128)} %bitcast.29, bf16[2,384,128]{2,1,0:T(8,128)(2,1)} %bitcast.23), custom_call_target="tpu_custom_call" | custom-call | tf_op jit(solution)/shard_map/triangle_updates/pallas_call | solution.py:493
  171.5 1.9 %copy.28 = f32[64,12,96]{2,0,1:T(8,128)} copy(f32[64,12,96]{2,1,0:T(8,128)} %triangle_updates.1) | data formatting | bytes 589824 | tf_op jit(solution)/shard_map/triangle_updates/pallas_call | solution.py:493
  (3 shorter events, 0.0 us)
Async XLA Ops:
  0.0 0.7 copy-start.5
  0.8 0.7 copy-start.4
  0.8 0.7 copy-start.3
  2.5 0.9 slice-start
  3.5 0.9 copy-start
  3.5 0.9 copy-start.1
  3.5 0.9 copy-start.2
  5.1 1.0 slice-start.1

commit v2 on v1

--- a/solution.py
+++ b/solution.py
@@ -29,13 +29,6 @@
         assert nz * rows == nx * cols and self.near * rows == cols
 
 
-def packed(geo, x):
-    lead = x.shape[:-2]
-    main = x[..., : geo.blocks, :]
-    rest = x[..., geo.blocks :, :].reshape(*lead, geo.blocks, geo.spare)
-    return jnp.concatenate([main, rest], axis=-1).reshape(*lead, geo.width)
-
-
 def lane_block(v, k):
     return v[:, k * LANES : (k + 1) * LANES]
 
@@ -71,11 +64,23 @@
 def kernel(
     geo,
     half,
-    z_ref,
+    pair_hbm,
+    flag_ref,
+    flags_ref,
+    gain_in_hbm,
+    proj_hbm,
+    gate_hbm,
+    gain_out_hbm,
+    out_hbm,
+    out_ref,
+    pair_ref,
+    gains,
+    proj_raw,
+    gate_raw,
+    out_raw,
+    weight_ref,
     mask_ref,
-    weight_ref,
-    out_ref,
-    z_next,
+    z_all,
     zn,
     tmp,
     gate,
@@ -98,6 +103,7 @@
     other_sem,
     z_sem,
     sent_sem,
+    load_sem,
 ):
     nz, nx = geo.nz, geo.nx
     me_z = lax.axis_index("gx")
@@ -146,21 +152,88 @@
             for h in range(2):
                 mat[lead, h, pl.ds(base + r, 1), :] = row[h : h + 1, :]
 
-    group = 4
     lag = 8
+    wide = geo.width
+
+    loads = [
+        pltpu.make_async_copy(src, dst, load_sem.at[i])
+        for i, (src, dst) in enumerate(
+            [
+                (pair_hbm, pair_ref),
+                (gain_in_hbm, gains.at[0]),
+                (gain_out_hbm, gains.at[1]),
+                (proj_hbm, proj_raw),
+                (gate_hbm, gate_raw),
+                (out_hbm, out_raw),
+            ]
+        )
+    ]
+    for load in loads:
+        load.start()
+    for load in loads[:3]:
+        load.wait()
+    for k in range(geo.blocks):
+        e, q = divmod(k, geo.pieces)
+        low = geo.spare * q
+        z_all[0, me_c, :, k * LANES : (k + 1) * LANES] = jnp.concatenate(
+            [pair_ref[:, k, :], pair_ref[:, geo.blocks + e, low : low + geo.spare]], axis=1
+        )
+    diagonal = lax.broadcasted_iota(jnp.int32, (half, half), 0) == lax.broadcasted_iota(
+        jnp.int32, (half, half), 1
+    )
+    columns = [
+        jnp.sum(jnp.where(diagonal, gains[kind, u : u + 1, :], 0.0), axis=1, keepdims=True)
+        for kind in range(2)
+        for u in range(2)
+    ]
+    lane = lax.broadcasted_iota(jnp.int32, (half, LANES), 1)
+    last = jnp.zeros((half, LANES), F32)
+    for i, column in enumerate(columns):
+        last = jnp.where(lane == i, column, last)
+    z_all[0, me_c, :, wide:] = last
+
+    flags = flags_ref[...].astype(F32)
+    near_flags = jnp.zeros((1, LANES), F32)
+    for x in range(nx):
+        own = jnp.where(me_x == x, 1.0, 0.0)
+        part = flags[:, geo.cols * x : geo.cols * (x + 1)]
+        near_flags += own * jnp.concatenate([part, jnp.zeros((1, geo.spare), F32)], axis=1)
+    row_flag = [flag_ref[me_z * geo.rows + r].astype(F32) for r in range(geo.rows)]
+    for k in range(geo.blocks):
+        mask_ref[:, k * LANES : (k + 1) * LANES] = block_of(
+            geo, lambda r: near_flags * row_flag[r], k
+        )
+
+    for load in loads[3:]:
+        load.wait()
+    for u in range(2):
+        raw = [proj_raw.at[u, p] for p in range(4)] + [gate_raw.at[u], out_raw.at[u]]
+        for p, ref in enumerate(raw):
+            weight_ref[u, p * half : (p + 1) * half, :] = ref[...].astype(F32).T.astype(BF16)
+
+    pl.semaphore_wait(barrier, nz - 1 + nx - 1 + 1)
+
+    def z_piece(u, i):
+        low = i * chunk
+        high = low + chunk + (LANES if u == 0 and i == geo.extra - 1 else 0)
+        part = z_all.at[u, me_c, :, low:high]
+        return copy_c(part, part, sent_sem.at[5, u], z_sem.at[u, i])
+
+    for i in reversed(range(geo.extra)):
+        z_piece(0, i).start()
 
     for u in range(2):
         weights = weight_ref.at[u]
         left_u, right_u, back_u = left_out.at[u], right_out.at[u], back_out.at[u]
 
-        gain_in = z_ref[:, geo.width + u : geo.width + u + 1]
-        for i, s in enumerate(chunks):
-            if u == 0:
-                z = z_ref[:, s]
-            else:
-                piece = z_next.at[me_c, :, s]
-                copy_c(piece, piece, sent_sem.at[5, 0], z_sem.at[i]).wait_recv()
-                z = jnp.concatenate([z_next[0, :, s], z_next[1, :, s]], axis=0)
+        for i in reversed(range(geo.extra)):
+            z_piece(u, i).wait_recv()
+            s = chunks[i]
+            if i == geo.extra - 1:
+                gain_in = jnp.concatenate(
+                    [z_all[0, c, :, wide + u : wide + u + 1] for c in range(2)], axis=0
+                )
+            z = jnp.concatenate([z_all[u, 0, :, s], z_all[u, 1, :, s]], axis=0)
             zn[:, s] = normed(z, gain_in)
 
         def project(first, out):
@@ -232,9 +305,6 @@
                     jnp.dot(weights[4 * half : 5 * half, :], zn[:, s], preferred_element_type=F32)
                 )
 
-        def left_base(k, s):
-            return (k if u == 0 else s) * geo.rows
-
         def take_left(k):
             s = far_first(k)
             slot = left_all.at[u, me_x, s]
@@ -244,7 +314,7 @@
                 copy_z(slot, slot, sent_sem.at[0, u], left_sem.at[u, me_x, s], s).wait_recv()
                 forward_left(slot, s)
 
-            store_rows(left_mat, me_x, left_base(k, s), left_all[u, me_x, s].astype(F32))
+            store_rows(left_mat, me_x, s * geo.rows, left_all[u, me_x, s].astype(F32))
 
         def take_left_x(k):
             s = far_first(k)
@@ -252,7 +322,7 @@
                 x = lax.rem(me_x + d, nx)
                 slot = left_all.at[u, x, s]
                 copy_x(slot, slot, sent_sem.at[2, u], left_sem.at[u, x, s], x).wait_recv()
-                store_rows(left_mat, x, left_base(k, s), left_all[u, x, s].astype(F32))
+                store_rows(left_mat, x, s * geo.rows, left_all[u, x, s].astype(F32))
 
         def wait_right(k, s):
             slot = right_in.at[u, s]
@@ -266,7 +336,7 @@
 
         def send_back(k):
             to = far_first(k)
-            base = left_base(k, to)
+            base = to * geo.rows
             for b in range(geo.blocks):
                 value = block_of(geo, functools.partial(block_row, base), b)
                 back_u[to, :, b * LANES : (b + 1) * LANES] = value.astype(BF16)
@@ -277,18 +347,41 @@
                     back_u.at[to], back_in.at[u, me_z], sent_sem.at[4, u], back_sem.at[u, me_z], to
                 ).start()
 
+        project(0, left_u)
+        send_left()
+        project(2 * half, right_u)
+        send_right()
         if u == 0:
-            project(2 * half, right_u)
-            pl.semaphore_wait(barrier, nz - 1 + nx - 1 + 1)
-            send_right()
             forward_right(right_u.at[me_z], me_z)
-            project(0, left_u)
-            send_left()
-            open_gate()
-
-            def take_right(k, _):
-                s = far_first(k)
-                wait_right(k, s)
+        open_gate()
+
+        def take_lefts(k, _):
+            take_left(k)
+
+            @pl.when(k >= lag)
+            def run():
+                take_left_x(k - lag)
+
+            return _
+
+        lax.fori_loop(0, nz, take_lefts, 0)
+
+        def take_right_x(k):
+            s = far_first(k)
+            at = s % geo.near
+
+            @pl.when(s // geo.near == me_x)
+            def run():
+                for d in range(1, nx):
+                    x = lax.rem(me_x + d, nx)
+                    slot = right_all.at[x, at]
+                    copy_x(slot, slot, sent_sem.at[3, 0], right_x_sem.at[x, at], x).wait_recv()
+                    store_rows(right_mat, x, at * geo.rows, right_all[x, at].astype(F32))
+
+        def take_right(k, _):
+            s = far_first(k)
+            wait_right(k, s)
+            if u == 0:
 
                 @pl.when(k < nz - 1)
                 def run():
@@ -300,94 +393,40 @@
                         right_mat, me_x, (s % geo.near) * geo.rows, right_in[0, s].astype(F32)
                     )
 
+                @pl.when(k >= lag)
+                def run_x():
+                    take_right_x(k - lag)
+
+            else:
+                store_rows(right_mat, 0, s * geo.rows, right_in[1, s].astype(F32))
+
+            @pl.when(k < lag)
+            def run_left():
+                take_left_x(nz - lag + k)
+
+            return _
+
+        lax.fori_loop(0, nz, take_right, 0)
+
+        if u == 0:
+
+            def take_last(k, _):
+                take_right_x(k)
                 return _
 
-            lax.fori_loop(0, nz, take_right, 0)
-
-            def take_group(g):
-                def take(i, _):
-                    take_left(g * group + i)
-                    return _
-
-                lax.fori_loop(0, group, take, 0)
-
-            take_group(0)
-
-            for d in range(1, nx):
-                x = lax.rem(me_x + d, nx)
-
-                def take_right_x(k, _):
-                    slot = right_all.at[x, k]
-                    copy_x(slot, slot, sent_sem.at[3, 0], right_x_sem.at[x, k], x).wait_recv()
-                    store_rows(right_mat, x, k * geo.rows, right_all[x, k].astype(F32))
-                    return _
-
-                lax.fori_loop(0, geo.near, take_right_x, 0)
-            take_group(1)
-
-            tall = group * geo.rows
-
-            def work(g, _):
-                @pl.when(g < nz // group - 2)
-                def run():
-                    take_group(g + 2)
-
-                def take_x(i, _):
-                    take_left_x(g * group + i)
-                    return _
-
-                lax.fori_loop(0, group, take_x, 0)
-                rows = pl.ds(pl.multiple_of(g * tall, tall), tall)
-                for h in range(2):
-                    total = jnp.zeros((tall, geo.cols), F32)
-                    for x in range(nx):
-                        total += lax.dot_general(
-                            left_mat[x, h, rows, :].astype(BF16),
-                            right_mat[x, h, : geo.cols, :].astype(BF16),
-                            (((1,), (1,)), ((), ())),
-                            preferred_element_type=F32,
-                        )
-                    product[h, rows, : geo.cols] = total
-
-                def send(i, _):
-                    send_back(g * group + i)
-                    return _
-
-                lax.fori_loop(0, group, send, 0)
-                return _
-
-            lax.fori_loop(0, nz // group, work, 0)
+            lax.fori_loop(nz - lag, nz, take_last, 0)
+
+            for h in range(2):
+                total = jnp.zeros((geo.res, geo.cols), F32)
+                for x in range(nx):
+                    total += lax.dot_general(
+                        left_mat[x, h].astype(BF16),
+                        right_mat[x, h, : geo.cols, :].astype(BF16),
+                        (((1,), (1,)), ((), ())),
+                        preferred_element_type=F32,
+                    )
+                product[h, :, : geo.cols] = total
         else:
-            project(0, left_u)
-            send_left()
-            project(2 * half, right_u)
-            send_right()
-            open_gate()
-
-            def take_lefts(k, _):
-                take_left(k)
-
-                @pl.when(k >= lag)
-                def run():
-                    take_left_x(k - lag)
-
-                return _
-
-            lax.fori_loop(0, nz, take_lefts, 0)
-
-            def take_right(k, _):
-                s = far_first(k)
-                wait_right(k, s)
-                store_rows(right_mat, 0, s * geo.rows, right_in[1, s].astype(F32))
-
-                @pl.when(k < lag)
-                def run():
-                    take_left_x(nz - lag + k)
-
-                return _
-
-            lax.fori_loop(0, nz, take_right, 0)
-
             for h in range(2):
                 right = right_mat[0, h].astype(BF16)
                 for x in range(nx):
@@ -399,11 +438,11 @@
                     )
                     product[h, geo.cols * x : geo.cols * (x + 1), :] = part[: geo.cols, :]
 
-            def send(k, _):
-                send_back(k)
-                return _
-
-            lax.fori_loop(0, nz, send, 0)
+        def send(k, _):
+            send_back(k)
+            return _
+
+        lax.fori_loop(0, nz, send, 0)
 
         def take_back(k, _):
             s = far_first(k)
@@ -427,20 +466,20 @@
 
         lax.fori_loop(0, nz, take_other, 0)
 
-        gain_out = z_ref[:, geo.width + 2 + u : geo.width + 3 + u]
-        for i, s in enumerate(chunks):
+        at = wide + 2 + u
+        gain_out = jnp.concatenate([z_all[0, c, :, at : at + 1] for c in range(2)], axis=0)
+        for i in reversed(range(geo.extra)):
+            s = chunks[i]
             values = jnp.concatenate(
                 [triangle[c, k, :, s] for c in range(2) for k in range(nz)], axis=0
             )
             tn = normed(values, gain_out)
             change = jnp.dot(weights[5 * half :, :], tn, preferred_element_type=F32)
+            value = z_all[u, me_c, :, s] + gate[:, s] * change
             if u == 0:
-                mine = z_ref[pl.ds(pl.multiple_of(me_c * half, half), half), s]
-                z_next[me_c, :, s] = mine + gate[:, s] * change
-                piece = z_next.at[me_c, :, s]
-                copy_c(piece, piece, sent_sem.at[5, 0], z_sem.at[i]).start()
+                z_all[1, me_c, :, s] = value
+                z_piece(1, i).start()
             else:
-                value = z_next[me_c, :, s] + gate[:, s] * change
                 lane = lax.broadcasted_iota(jnp.int32, (half, LANES), 1)
                 row = jnp.zeros((half, LANES), F32)
                 for q in range(geo.pieces):
@@ -451,7 +490,7 @@
                     row = jnp.where((lane >= low) & (lane < low + geo.spare), moved, row)
                 out_ref[:, geo.blocks + i, :] = row[:, : geo.cols]
 
-    any_sem = z_sem.at[0]
+    any_sem = z_sem.at[0, 0]
     for u in range(2):
         many = left_out.at[u, pl.ds(0, nz - 1)]
         copy_z(many, many, sent_sem.at[0, u], any_sem, me_z).wait_send()
@@ -464,7 +503,9 @@
         copy_c(every, every, sent_sem.at[6, u], any_sem).wait_send()
     away = left_out.at[0, pl.ds(0, nz - geo.near)]
     copy_x(away, away, sent_sem.at[3, 0], any_sem, me_x).wait_send()
-    copy_c(z_next.at[me_c], z_next.at[me_c], sent_sem.at[5, 0], any_sem).wait_send()
+    for u in range(2):
+        part = z_all.at[u, me_c, :, : wide + (LANES if u == 0 else 0)]
+        copy_c(part, part, sent_sem.at[5, u], any_sem).wait_send()
 
 
 def per_device(
@@ -472,31 +513,34 @@
 ):
     half = pair.shape[0]
     full = 2 * half
-    row_start = lax.axis_index("gx") * geo.rows
-    col_start = lax.axis_index("gy") * geo.cols
-    row_flags = lax.dynamic_slice_in_dim(residue_mask, row_start, geo.rows).astype(F32)
-    col_flags = lax.dynamic_slice_in_dim(residue_mask, col_start, geo.cols).astype(F32)
-    mask = packed(geo, row_flags[:, None] * col_flags[None, :])[None, :]
-    gains = jnp.concatenate([norm_in_gain, norm_out_gain], axis=0).T
-    gains = jnp.pad(gains, ((0, 0), (0, LANES - 4)))
-    z = jnp.concatenate([packed(geo, pair), gains], axis=1)
-    z = lax.all_gather(z, "gz", axis=0, tiled=True)
-    weights = jnp.concatenate(
-        [proj_weight, gate_weight[:, None], out_weight[:, None]], axis=1
-    )
-    weights = jnp.swapaxes(weights, 2, 3).reshape(2, 6 * half, full)
-
     nz, nx = geo.nz, geo.nx
     vmem = pltpu.VMEM
     message = (2, geo.width)
     dma = pltpu.SemaphoreType.DMA
+    hbm = pl.BlockSpec(memory_space=pl.ANY)
     return pl.pallas_call(
         functools.partial(kernel, geo, half),
         out_shape=jax.ShapeDtypeStruct(pair.shape, F32),
-        in_specs=[pl.BlockSpec(memory_space=vmem)] * 3,
+        in_specs=[
+            hbm,
+            pl.BlockSpec(memory_space=pltpu.SMEM),
+            pl.BlockSpec(memory_space=vmem),
+            hbm,
+            hbm,
+            hbm,
+            hbm,
+            hbm,
+        ],
         out_specs=pl.BlockSpec(memory_space=vmem),
         scratch_shapes=[
-            vmem((2, half, geo.width), F32),
+            vmem(pair.shape, F32),
+            vmem((2, *norm_in_gain.shape), F32),
+            vmem(proj_weight.shape, BF16),
+            vmem(gate_weight.shape, BF16),
+            vmem(out_weight.shape, BF16),
+            vmem((2, 6 * half, full), BF16),
+            vmem((1, geo.width), F32),
+            vmem((2, 2, half, geo.width + LANES), F32),
             vmem((full, geo.width), BF16),
             vmem((half, geo.width), F32),
             vmem((half, geo.width), F32),
@@ -517,14 +561,24 @@
             dma((nx, geo.near)),
             dma((2, nz)),
             dma((2, nz)),
-            dma((geo.extra,)),
+            dma((2, geo.extra)),
             dma((7, 2)),
+            dma((6,)),
         ],
         compiler_params=pltpu.CompilerParams(
             collective_id=0, has_side_effects=True, vmem_limit_bytes=60 * 1024 * 1024
         ),
         name="triangle_updates",
-    )(z, mask, weights)
+    )(
+        pair,
+        residue_mask,
+        residue_mask[None, :],
+        norm_in_gain,
+        proj_weight,
+        gate_weight,
+        norm_out_gain,
+        out_weight,
+    )
 
 
 def solution(mesh):

time: 174 us -> 183 us (1.052)
  Pallas kernels: 122 us -> 174 us
  blocking collectives: 43.5 us -> 0 us
    pallas_call x1, Pallas kernels: 122 us -> 174 us  [per_device(): pl.pallas_call(functools.partial(kernel, geo, half), out_shape=jax.ShapeD...]
    all_gather x1 -> x0, blocking collectives: 43.5 us -> none  [per_device(): z = lax.all_gather(z, 'gz', axis=0, tiled=True)]
    unnamed x14 -> x8, local copies, waits for them, and re-layouts: 2.81 us -> 4.85 us
    slice x5 -> x0, local copies, waits for them, and re-layouts: 1.86 us -> none  [the longest x2 0.96 us: packed(): main = x[..., :geo.blocks, :]]
where the time goes in v2:
time: 183 us; the launch traced here: 182 us
  Pallas kernels  174 us (95%)
  local copies, waits for them, and re-layouts  8.04 us (4%)
    pallas_call x1, Pallas kernels, per_device(): pl.pallas_call(functools.partial(kernel, geo, half), out_shape=jax.ShapeD...  174 us
    unnamed x8, local copies, waits for them, and re-layouts  4.85 us

profile of v2, /device:TPU:33, one launch (start us, length us, event | category | flops | bytes accessed | tf_op | source)
XLA Modules:
  0.0 182.4 jit_solution(5398153846365921606)
XLA Ops:
  0.0 0.0 copy-start.1
  0.0 0.0 copy-start
  0.0 1.3 broadcast_in_dim.3.flags_ref
  1.3 1.5 copy.10.gate_hbm
  2.8 1.5 copy.11.out_hbm
  4.3 0.0 copy-done.1
  4.3 0.9 copy.9.proj_hbm
  5.1 0.0 copy-done
  5.1 1.0 copy.8.pair_hbm
  6.1 174.3 %triangle_updates.1 = f32[64,12,96]{2,1,0:T(8,128)} custom-call(f32[64,12,96]{2,1,0:T(8,128)} %copy.8.pair_hbm, s32[384]{0:T(512)} %flag_ref.1, s32[1,384]{1,0:T(1,128)} %broadcast_in_dim.3.flags_ref, f32[2,64]{1,0:T(2,128)} %gain_in_hbm.1, bf16[2,4,128,64]{3,2,1,0:T(8,128)(2,1)} %copy.9.proj_hbm, bf16[2,128,64]{2,1,0:T(8,128)(2,1)} %copy.10.gate_hbm, ...), custom_call_target="tpu_custom_call" | custom-call | tf_op jit(solution)/shard_map/triangle_updates/pallas_call | solution.py:521
  180.5 1.9 %copy.12 = f32[64,12,96]{2,0,1:T(8,128)} copy(f32[64,12,96]{2,1,0:T(8,128)} %triangle_updates.1) | data formatting | bytes 589824 | tf_op jit(solution)/shard_map/triangle_updates/pallas_call | solution.py:521
Async XLA Ops:
  0.0 4.3 %copy-start.1 = (bf16[2,4,128,64]{2,3,1,0:T(8,128)(2,1)S(1)}, bf16[2,4,128,64]{2,3,1,0:T(8,128)(2,1)}, u32[]{:S(2)}) copy-start(bf16[2,4,128,64]{2,3,1,0:T(8,128)(2,1)} %param.10) | copy-start | bytes 393220
  0.0 5.1 %copy-start = (f32[64,12,96]{2,0,1:T(8,128)S(1)}, f32[64,12,96]{2,0,1:T(8,128)}, u32[]{:S(2)}) copy-start(f32[64,12,96]{2,0,1:T(8,128)} %param.7) | copy-start | bytes 884740

commit v3 on v2

--- a/solution.py
+++ b/solution.py
@@ -66,7 +66,6 @@
     half,
     pair_hbm,
     flag_ref,
-    flags_ref,
     gain_in_hbm,
     proj_hbm,
     gate_hbm,
@@ -75,10 +74,9 @@
     out_ref,
     pair_ref,
     gains,
-    proj_raw,
-    gate_raw,
-    out_raw,
-    weight_ref,
+    proj_ref,
+    gate_ref,
+    out_weight_ref,
     mask_ref,
     z_all,
     zn,
@@ -162,9 +160,9 @@
                 (pair_hbm, pair_ref),
                 (gain_in_hbm, gains.at[0]),
                 (gain_out_hbm, gains.at[1]),
-                (proj_hbm, proj_raw),
-                (gate_hbm, gate_raw),
-                (out_hbm, out_raw),
+                (proj_hbm, proj_ref),
+                (gate_hbm, gate_ref),
+                (out_hbm, out_weight_ref),
             ]
         )
     ]
@@ -176,7 +174,7 @@
         e, q = divmod(k, geo.pieces)
         low = geo.spare * q
         z_all[0, me_c, :, k * LANES : (k + 1) * LANES] = jnp.concatenate(
-            [pair_ref[:, k, :], pair_ref[:, geo.blocks + e, low : low + geo.spare]], axis=1
+            [pair_ref[k], pair_ref[geo.blocks + e, :, low : low + geo.spare]], axis=1
         )
     diagonal = lax.broadcasted_iota(jnp.int32, (half, half), 0) == lax.broadcasted_iota(
         jnp.int32, (half, half), 1
@@ -192,12 +190,11 @@
         last = jnp.where(lane == i, column, last)
     z_all[0, me_c, :, wide:] = last
 
-    flags = flags_ref[...].astype(F32)
+    near_lane = lax.broadcasted_iota(jnp.int32, (1, LANES), 1)
     near_flags = jnp.zeros((1, LANES), F32)
-    for x in range(nx):
-        own = jnp.where(me_x == x, 1.0, 0.0)
-        part = flags[:, geo.cols * x : geo.cols * (x + 1)]
-        near_flags += own * jnp.concatenate([part, jnp.zeros((1, geo.spare), F32)], axis=1)
+    for t in range(geo.cols):
+        flag = flag_ref[me_x * geo.cols + t].astype(F32)
+        near_flags = jnp.where(near_lane == t, flag, near_flags)
     row_flag = [flag_ref[me_z * geo.rows + r].astype(F32) for r in range(geo.rows)]
     for k in range(geo.blocks):
         mask_ref[:, k * LANES : (k + 1) * LANES] = block_of(
@@ -206,10 +203,6 @@
 
     for load in loads[3:]:
         load.wait()
-    for u in range(2):
-        raw = [proj_raw.at[u, p] for p in range(4)] + [gate_raw.at[u], out_raw.at[u]]
-        for p, ref in enumerate(raw):
-            weight_ref[u, p * half : (p + 1) * half, :] = ref[...].astype(F32).T.astype(BF16)
 
     pl.semaphore_wait(barrier, nz - 1 + nx - 1 + 1)
 
@@ -223,7 +216,6 @@
         z_piece(0, i).start()
 
     for u in range(2):
-        weights = weight_ref.at[u]
         left_u, right_u, back_u = left_out.at[u], right_out.at[u], back_out.at[u]
 
         for i in reversed(range(geo.extra)):
@@ -238,10 +230,11 @@
 
         def project(first, out):
             for s in chunks:
-                both = jnp.dot(
-                    weights[first : first + 2 * half, :], zn[:, s], preferred_element_type=F32
+                opening, value = (
+                    jnp.dot(proj_ref[u, first + i], zn[:, s], preferred_element_type=F32)
+                    for i in range(2)
                 )
-                tmp[:, s] = jax.nn.sigmoid(both[:half]) * both[half:] * mask_ref[:, s]
+                tmp[:, s] = jax.nn.sigmoid(opening) * value * mask_ref[:, s]
             for k in range(nz):
                 out[k] = tmp[2 * k : 2 * k + 2, :].astype(BF16)
 
@@ -302,7 +295,7 @@
         def open_gate():
             for s in chunks:
                 gate[:, s] = jax.nn.sigmoid(
-                    jnp.dot(weights[4 * half : 5 * half, :], zn[:, s], preferred_element_type=F32)
+                    jnp.dot(gate_ref[u], zn[:, s], preferred_element_type=F32)
                 )
 
         def take_left(k):
@@ -349,7 +342,7 @@
 
         project(0, left_u)
         send_left()
-        project(2 * half, right_u)
+        project(2, right_u)
         send_right()
         if u == 0:
             forward_right(right_u.at[me_z], me_z)
@@ -474,7 +467,7 @@
                 [triangle[c, k, :, s] for c in range(2) for k in range(nz)], axis=0
             )
             tn = normed(values, gain_out)
-            change = jnp.dot(weights[5 * half :, :], tn, preferred_element_type=F32)
+            change = jnp.dot(out_weight_ref[u], tn, preferred_element_type=F32)
             value = z_all[u, me_c, :, s] + gate[:, s] * change
             if u == 0:
                 z_all[1, me_c, :, s] = value
@@ -484,11 +477,11 @@
                 row = jnp.zeros((half, LANES), F32)
                 for q in range(geo.pieces):
                     block = lane_block(value, q)
-                    out_ref[:, i * geo.pieces + q, :] = block[:, : geo.cols]
+                    out_ref[i * geo.pieces + q] = block[:, : geo.cols]
                     low = geo.spare * q
                     moved = pltpu.roll(block, (low - geo.cols) % LANES, 1)
                     row = jnp.where((lane >= low) & (lane < low + geo.spare), moved, row)
-                out_ref[:, geo.blocks + i, :] = row[:, : geo.cols]
+                out_ref[geo.blocks + i] = row[:, : geo.cols]
 
     any_sem = z_sem.at[0, 0]
     for u in range(2):
@@ -518,13 +511,16 @@
     message = (2, geo.width)
     dma = pltpu.SemaphoreType.DMA
     hbm = pl.BlockSpec(memory_space=pl.ANY)
-    return pl.pallas_call(
+    pair = jnp.swapaxes(pair, 0, 1)
+    proj_weight = jnp.swapaxes(proj_weight, 2, 3)
+    gate_weight = jnp.swapaxes(gate_weight, 1, 2)
+    out_weight = jnp.swapaxes(out_weight, 1, 2)
+    result = pl.pallas_call(
         functools.partial(kernel, geo, half),
         out_shape=jax.ShapeDtypeStruct(pair.shape, F32),
         in_specs=[
             hbm,
             pl.BlockSpec(memory_space=pltpu.SMEM),
-            pl.BlockSpec(memory_space=vmem),
             hbm,
             hbm,
             hbm,
@@ -538,7 +534,6 @@
             vmem(proj_weight.shape, BF16),
             vmem(gate_weight.shape, BF16),
             vmem(out_weight.shape, BF16),
-            vmem((2, 6 * half, full), BF16),
             vmem((1, geo.width), F32),
             vmem((2, 2, half, geo.width + LANES), F32),
             vmem((full, geo.width), BF16),
@@ -572,13 +567,13 @@
     )(
         pair,
         residue_mask,
-        residue_mask[None, :],
         norm_in_gain,
         proj_weight,
         gate_weight,
         norm_out_gain,
         out_weight,
     )
+    return jnp.swapaxes(result, 0, 1)
 
 
 def solution(mesh):

time: 183 us -> 175 us (0.956)
  local copies, waits for them, and re-layouts: 8.04 us -> 1.77 us
    unnamed x8 -> x1, local copies, waits for them, and re-layouts: 4.85 us -> 1.77 us
    pallas_call x1 -> x0, local copies, waits for them, and re-layouts: 1.92 us -> none  [per_device(): pl.pallas_call(functools.partial(kernel, geo, half), out_shape=jax.ShapeD...]
where the time goes in v3:
time: 175 us
  Pallas kernels  174 us (99%)
  local copies, waits for them, and re-layouts  1.77 us (1%)
    pallas_call x1, Pallas kernels, per_device(): pl.pallas_call(functools.partial(kernel, geo, half), out_shape=jax.ShapeD...  174 us

profile of v3, /device:TPU:33, one launch (start us, length us, event | category | flops | bytes accessed | tf_op | source)
XLA Modules:
  0.0 175.3 jit_solution(902412992103890233)
XLA Ops:
  0.0 173.5 %triangle_updates.1 = f32[12,64,96]{2,1,0:T(8,128)} custom-call(f32[12,64,96]{2,1,0:T(8,128)} %bitcast.6, s32[384]{0:T(512)} %flag_ref.1, f32[2,64]{1,0:T(2,128)} %gain_in_hbm.1, bf16[2,4,64,128]{3,2,1,0:T(8,128)(2,1)} %bitcast.7, bf16[2,64,128]{2,1,0:T(8,128)(2,1)} %bitcast.8, f32[2,64]{1,0:T(2,128)} %gain_out_hbm.1, bf16[2,64,128]{2,1,0:T(8,128)(2,1)} %bitcast.9), custom_call_target="tpu_custom_call" | custom-call | tf_op jit(solution)/shard_map/triangle_updates/pallas_call | solution.py:518
  173.5 1.8 %copy.9 = f32[64,12,96]{2,0,1:T(8,128)} copy(f32[64,12,96]{2,0,1:T(8,128)} %bitcast.5) | data formatting | bytes 589824

commit v4 on v3

--- a/solution.py
+++ b/solution.py
@@ -102,6 +102,8 @@
     z_sem,
     sent_sem,
     load_sem,
+    up_sem,
+    down_sem,
 ):
     nz, nx = geo.nz, geo.nx
     me_z = lax.axis_index("gx")
@@ -113,13 +115,10 @@
 
     barrier = pltpu.get_barrier_semaphore()
 
-    def signal_z(k, _):
-        pl.semaphore_signal(
-            barrier, inc=1, device_id={"gx": lax.rem(me_z + 1 + k, nz)}, device_id_type=MESH
-        )
-        return _
-
-    lax.fori_loop(0, nz - 1, signal_z, 0)
+    after = lax.rem(me_z + 1, nz)
+    before = lax.rem(me_z + nz - 1, nz)
+    for neighbour in (before, after):
+        pl.semaphore_signal(barrier, inc=1, device_id={"gx": neighbour}, device_id_type=MESH)
     for k in range(1, nx):
         pl.semaphore_signal(
             barrier, inc=1, device_id={"gy": lax.rem(me_x + k, nx)}, device_id_type=MESH
@@ -150,7 +149,7 @@
             for h in range(2):
                 mat[lead, h, pl.ds(base + r, 1), :] = row[h : h + 1, :]
 
-    lag = 8
+    lag = 6
     wide = geo.width
 
     loads = [
@@ -204,7 +203,7 @@
     for load in loads[3:]:
         load.wait()
 
-    pl.semaphore_wait(barrier, nz - 1 + nx - 1 + 1)
+    pl.semaphore_wait(barrier, 2 + nx - 1 + 1)
 
     def z_piece(u, i):
         low = i * chunk
@@ -214,6 +213,52 @@
 
     for i in reversed(range(geo.extra)):
         z_piece(0, i).start()
+
+    middle = nz // 2
+    early = jnp.where(me_z >= middle, middle, jnp.where(me_z == 0, middle - 1, me_z))
+    later = jnp.where(me_z < middle, middle, nz - 1 - me_z)
+    up_limit = jnp.where(after >= middle, middle, middle - 1)
+    down_limit = jnp.where(before < middle, middle, middle - 1)
+    below = me_z < middle
+
+    def hear_up(j):
+        @pl.when(j > 1)
+        def run():
+            pl.semaphore_wait(up_sem.at[j], 1)
+
+        @pl.when(j < up_limit)
+        def relay():
+            pl.semaphore_signal(up_sem.at[j + 1], inc=1, device_id={"gx": after}, device_id_type=MESH)
+
+    def hear_down(j):
+        @pl.when(j > 1)
+        def run():
+            pl.semaphore_wait(down_sem.at[j], 1)
+
+        @pl.when(j < down_limit)
+        def relay():
+            pl.semaphore_signal(
+                down_sem.at[j + 1], inc=1, device_id={"gx": before}, device_id_type=MESH
+            )
+
+    def hear_early(j, _):
+        hear_up(j)
+        return _
+
+    lax.fori_loop(1, early + 1, hear_early, 0)
+
+    def by_word(n):
+        crossed = n - early - later
+        s = jnp.where(
+            n < early,
+            me_z - 1 - n,
+            jnp.where(
+                n < early + later,
+                me_z + 1 + n - early,
+                jnp.where(below, me_z - early - 1 - crossed, me_z + later + 1 + crossed),
+            ),
+        )
+        return jnp.where(n == nz - 1, me_z, lax.rem(s + nz, nz))
 
     for u in range(2):
         left_u, right_u, back_u = left_out.at[u], right_out.at[u], back_out.at[u]
@@ -261,36 +306,23 @@
                     target,
                 ).start()
 
-        def send_left():
-            def send(k, _):
-                to = far_first(k)
-                copy_z(
-                    left_u.at[to],
-                    left_all.at[u, me_x, me_z],
-                    sent_sem.at[0, u],
-                    left_sem.at[u, me_x, me_z],
-                    to,
-                ).start()
-                return _
-
-            lax.fori_loop(0, nz - 1, send, 0)
-            forward_left(left_u.at[me_z], me_z)
-            left_all[u, me_x, me_z] = left_u[me_z]
-
-        def send_right():
-            def send(k, _):
-                to = far_first(k)
-                copy_z(
-                    right_u.at[to],
-                    right_in.at[u, me_z],
-                    sent_sem.at[1, u],
-                    right_sem.at[u, me_z],
-                    to,
-                ).start()
-                return _
-
-            lax.fori_loop(0, nz - 1, send, 0)
-            right_in[u, me_z] = right_u[me_z]
+        def send_left(to):
+            copy_z(
+                left_u.at[to],
+                left_all.at[u, me_x, me_z],
+                sent_sem.at[0, u],
+                left_sem.at[u, me_x, me_z],
+                to,
+            ).start()
+
+        def send_right(to):
+            copy_z(
+                right_u.at[to],
+                right_in.at[u, me_z],
+                sent_sem.at[1, u],
+                right_sem.at[u, me_z],
+                to,
+            ).start()
 
         def open_gate():
             for s in chunks:
@@ -298,8 +330,10 @@
                     jnp.dot(gate_ref[u], zn[:, s], preferred_element_type=F32)
                 )
 
+        source = by_word if u == 0 else far_first
+
         def take_left(k):
-            s = far_first(k)
+            s = source(k)
             slot = left_all.at[u, me_x, s]
 
             @pl.when(k < nz - 1)
@@ -310,7 +344,7 @@
             store_rows(left_mat, me_x, s * geo.rows, left_all[u, me_x, s].astype(F32))
 
         def take_left_x(k):
-            s = far_first(k)
+            s = source(k)
             for d in range(1, nx):
                 x = lax.rem(me_x + d, nx)
                 slot = left_all.at[u, x, s]
@@ -340,27 +374,8 @@
                     back_u.at[to], back_in.at[u, me_z], sent_sem.at[4, u], back_sem.at[u, me_z], to
                 ).start()
 
-        project(0, left_u)
-        send_left()
-        project(2, right_u)
-        send_right()
-        if u == 0:
-            forward_right(right_u.at[me_z], me_z)
-        open_gate()
-
-        def take_lefts(k, _):
-            take_left(k)
-
-            @pl.when(k >= lag)
-            def run():
-                take_left_x(k - lag)
-
-            return _
-
-        lax.fori_loop(0, nz, take_lefts, 0)
-
         def take_right_x(k):
-            s = far_first(k)
+            s = source(k)
             at = s % geo.near
 
             @pl.when(s // geo.near == me_x)
@@ -371,10 +386,43 @@
                     copy_x(slot, slot, sent_sem.at[3, 0], right_x_sem.at[x, at], x).wait_recv()
                     store_rows(right_mat, x, at * geo.rows, right_all[x, at].astype(F32))
 
-        def take_right(k, _):
-            s = far_first(k)
-            wait_right(k, s)
-            if u == 0:
+        project(0, left_u)
+        forward_left(left_u.at[me_z], me_z)
+        left_all[u, me_x, me_z] = left_u[me_z]
+        if u == 0:
+            project(2, right_u)
+            forward_right(right_u.at[me_z], me_z)
+            right_in[u, me_z] = right_u[me_z]
+
+            def send_both(to):
+                to = lax.rem(to + nz, nz)
+                send_left(to)
+                send_right(to)
+
+            def send_early(n, _):
+                send_both(me_z - early + n)
+                return _
+
+            def send_down(j, _):
+                hear_down(j)
+                send_both(me_z + j)
+                return _
+
+            def send_up(j, _):
+                hear_up(j)
+                send_both(me_z - j)
+                return _
+
+            lax.fori_loop(0, early, send_early, 0)
+            open_gate()
+            lax.fori_loop(1, later + 1, send_down, 0)
+            lax.fori_loop(jnp.where(below, early + 1, middle), middle, send_up, 0)
+            lax.fori_loop(jnp.where(below, middle, later + 1), middle, send_down, 0)
+
+            def take_both(k, _):
+                s = source(k)
+                take_left(k)
+                wait_right(k, s)
 
                 @pl.when(k < nz - 1)
                 def run():
@@ -388,22 +436,56 @@
 
                 @pl.when(k >= lag)
                 def run_x():
+                    take_left_x(k - lag)
                     take_right_x(k - lag)
 
-            else:
+                return _
+
+            lax.fori_loop(0, nz, take_both, 0)
+        else:
+
+            def send_lefts(k, _):
+                send_left(far_first(k))
+                return _
+
+            def send_rights(k, _):
+                send_right(far_first(k))
+                return _
+
+            lax.fori_loop(0, nz - 1, send_lefts, 0)
+            project(2, right_u)
+            lax.fori_loop(0, nz - 1, send_rights, 0)
+            right_in[u, me_z] = right_u[me_z]
+            open_gate()
+
+            def take_lefts(k, _):
+                take_left(k)
+
+                @pl.when(k >= lag)
+                def run():
+                    take_left_x(k - lag)
+
+                return _
+
+            lax.fori_loop(0, nz, take_lefts, 0)
+
+            def take_rights(k, _):
+                s = source(k)
+                wait_right(k, s)
                 store_rows(right_mat, 0, s * geo.rows, right_in[1, s].astype(F32))
 
-            @pl.when(k < lag)
-            def run_left():
-                take_left_x(nz - lag + k)
-
-            return _
-
-        lax.fori_loop(0, nz, take_right, 0)
+                @pl.when(k < lag)
+                def run_left():
+                    take_left_x(nz - lag + k)
+
+                return _
+
+            lax.fori_loop(0, nz, take_rights, 0)
 
         if u == 0:
 
             def take_last(k, _):
+                take_left_x(k)
                 take_right_x(k)
                 return _
 
@@ -559,6 +641,8 @@
             dma((2, geo.extra)),
             dma((7, 2)),
             dma((6,)),
+            pltpu.SemaphoreType.REGULAR((nz // 2 + 1,)),
+            pltpu.SemaphoreType.REGULAR((nz // 2 + 1,)),
         ],
         compiler_params=pltpu.CompilerParams(
             collective_id=0, has_side_effects=True, vmem_limit_bytes=60 * 1024 * 1024

time: 175 us -> 191 us (1.091)
  Pallas kernels: 174 us -> 189 us
    pallas_call x1, Pallas kernels: 174 us -> 189 us  [per_device(): pl.pallas_call(functools.partial(kernel, geo, half), out_shape=jax.ShapeD...]
where the time goes in v4:
time: 191 us
  Pallas kernels  189 us (99%)
    pallas_call x1, Pallas kernels, per_device(): pl.pallas_call(functools.partial(kernel, geo, half), out_shape=jax.ShapeD...  189 us

profile of v4, /device:TPU:33, one launch (start us, length us, event | category | flops | bytes accessed | tf_op | source)
XLA Modules:
  0.0 190.5 jit_solution(14545430577354896599)
XLA Ops:
  0.0 188.8 %triangle_updates.1 = f32[12,64,96]{2,1,0:T(8,128)} custom-call(f32[12,64,96]{2,1,0:T(8,128)} %bitcast.6, s32[384]{0:T(512)} %flag_ref.1, f32[2,64]{1,0:T(2,128)} %gain_in_hbm.1, bf16[2,4,64,128]{3,2,1,0:T(8,128)(2,1)} %bitcast.7, bf16[2,64,128]{2,1,0:T(8,128)(2,1)} %bitcast.8, f32[2,64]{1,0:T(2,128)} %gain_out_hbm.1, bf16[2,64,128]{2,1,0:T(8,128)(2,1)} %bitcast.9), custom_call_target="tpu_custom_call" | custom-call | tf_op jit(solution)/shard_map/triangle_updates/pallas_call | solution.py:600
  188.8 1.8 copy.9

commit v5 on v4

--- a/solution.py
+++ b/solution.py
@@ -215,11 +215,13 @@
         z_piece(0, i).start()
 
     middle = nz // 2
-    early = jnp.where(me_z >= middle, middle, jnp.where(me_z == 0, middle - 1, me_z))
-    later = jnp.where(me_z < middle, middle, nz - 1 - me_z)
-    up_limit = jnp.where(after >= middle, middle, middle - 1)
-    down_limit = jnp.where(before < middle, middle, middle - 1)
-    below = me_z < middle
+    place = before
+    early = jnp.where(place >= middle, middle, jnp.where(place == 0, middle - 1, place))
+    later = jnp.where(place < middle, middle, nz - 1 - place)
+    up_limit = jnp.where(me_z >= middle, middle, middle - 1)
+    down_limit = jnp.where(lax.rem(place + nz - 1, nz) < middle, middle, middle - 1)
+    below = place < middle
+    at_end = later <= 4
 
     def hear_up(j):
         @pl.when(j > 1)
@@ -245,7 +247,12 @@
         hear_up(j)
         return _
 
+    def hear_later(j, _):
+        hear_down(j)
+        return _
+
     lax.fori_loop(1, early + 1, hear_early, 0)
+    lax.fori_loop(1, jnp.where(at_end, later + 1, 1), hear_later, 0)
 
     def by_word(n):
         crossed = n - early - later
@@ -399,26 +406,6 @@
                 send_left(to)
                 send_right(to)
 
-            def send_early(n, _):
-                send_both(me_z - early + n)
-                return _
-
-            def send_down(j, _):
-                hear_down(j)
-                send_both(me_z + j)
-                return _
-
-            def send_up(j, _):
-                hear_up(j)
-                send_both(me_z - j)
-                return _
-
-            lax.fori_loop(0, early, send_early, 0)
-            open_gate()
-            lax.fori_loop(1, later + 1, send_down, 0)
-            lax.fori_loop(jnp.where(below, early + 1, middle), middle, send_up, 0)
-            lax.fori_loop(jnp.where(below, middle, later + 1), middle, send_down, 0)
-
             def take_both(k, _):
                 s = source(k)
                 take_left(k)
@@ -441,7 +428,41 @@
 
                 return _
 
-            lax.fori_loop(0, nz, take_both, 0)
+            def send_early(n, _):
+                send_both(me_z - early + n)
+                return _
+
+            between = jnp.maximum(jnp.minimum(later, early) - 2, 0) * jnp.minimum(place, 1)
+
+            def send_later(j, _):
+                @pl.when(jnp.logical_not(at_end))
+                def run():
+                    hear_down(j)
+
+                send_both(me_z + j)
+
+                @pl.when((j > 2) & (j - 3 < between))
+                def run_take():
+                    take_both(j - 3, 0)
+
+                return _
+
+            def send_down(j, _):
+                hear_down(j)
+                send_both(me_z + j)
+                return _
+
+            def send_up(j, _):
+                hear_up(j)
+                send_both(me_z - j)
+                return _
+
+            lax.fori_loop(0, early, send_early, 0)
+            open_gate()
+            lax.fori_loop(1, later + 1, send_later, 0)
+            lax.fori_loop(jnp.where(below, early + 1, middle), middle, send_up, 0)
+            lax.fori_loop(jnp.where(below, middle, later + 1), middle, send_down, 0)
+            lax.fori_loop(between, nz, take_both, 0)
         else:
 
             def send_lefts(k, _):

time: 191 us -> 177 us (0.927)
  Pallas kernels: 189 us -> 174 us
    pallas_call x1, Pallas kernels: 189 us -> 174 us  [per_device(): pl.pallas_call(functools.partial(kernel, geo, half), out_shape=jax.ShapeD...]
where the time goes in v5:
time: 177 us; the launch traced here: 176 us
  Pallas kernels  174 us (98%)
  local copies, waits for them, and re-layouts  1.77 us (1%)
    pallas_call x1, Pallas kernels, per_device(): pl.pallas_call(functools.partial(kernel, geo, half), out_shape=jax.ShapeD...  174 us

profile of v5, /device:TPU:33, one launch (start us, length us, event | category | flops | bytes accessed | tf_op | source)
XLA Modules:
  0.0 175.7 jit_solution(7395018286844202226)
XLA Ops:
  0.0 174.0 %triangle_updates.1 = f32[12,64,96]{2,1,0:T(8,128)} custom-call(f32[12,64,96]{2,1,0:T(8,128)} %bitcast.6, s32[384]{0:T(512)} %flag_ref.1, f32[2,64]{1,0:T(2,128)} %gain_in_hbm.1, bf16[2,4,64,128]{3,2,1,0:T(8,128)(2,1)} %bitcast.7, bf16[2,64,128]{2,1,0:T(8,128)(2,1)} %bitcast.8, f32[2,64]{1,0:T(2,128)} %gain_out_hbm.1, bf16[2,64,128]{2,1,0:T(8,128)(2,1)} %bitcast.9), custom_call_target="tpu_custom_call" | custom-call | tf_op jit(solution)/shard_map/triangle_updates/pallas_call | solution.py:621
  174.0 1.8 %copy.9 = f32[64,12,96]{2,0,1:T(8,128)} copy(f32[64,12,96]{2,0,1:T(8,128)} %bitcast.5) | data formatting | bytes 589824

commit v6 on v3

--- a/solution.py
+++ b/solution.py
@@ -25,7 +25,7 @@
         self.res = nz * rows
         self.near = cols // rows
         assert self.blocks * LANES == rows * cols
-        assert self.extra * self.pieces == self.blocks
+        assert self.extra * self.pieces == self.blocks and nz % 4 == 0
         assert nz * rows == nx * cols and self.near * rows == cols
 
 
@@ -130,6 +130,22 @@
         m = (k + 1) // 2
         return lax.rem(me_z + nz // 2 + m * (1 - 2 * (k % 2)), nz)
 
+    def team(k):
+        return (k + 3) // 4
+
+    def wait_team(k, copy_of, last):
+        @pl.when(k == 0)
+        def run_first():
+            copy_of(left_out.at[0, pl.ds(0, 1)]).wait_recv()
+
+        @pl.when((k % 4 == 1) & (k < nz - 3))
+        def run_full():
+            copy_of(left_out.at[0, pl.ds(0, 4)]).wait_recv()
+
+        @pl.when(k == nz - 3)
+        def run_last():
+            copy_of(left_out.at[0, pl.ds(0, last)]).wait_recv()
+
     def copy_z(src, dst, send, recv, to):
         return pltpu.make_async_remote_copy(
             src_ref=src, dst_ref=dst, send_sem=send, recv_sem=recv, device_id={"gx": to}, device_id_type=MESH
@@ -238,14 +254,14 @@
             for k in range(nz):
                 out[k] = tmp[2 * k : 2 * k + 2, :].astype(BF16)
 
-        def forward_left(src, s):
-            for k in range(1, nx):
+        def forward_left(src, s, k):
+            for d in range(1, nx):
                 copy_x(
                     src,
                     left_all.at[u, me_x, s],
                     sent_sem.at[2, u],
-                    left_sem.at[u, me_x, s],
-                    lax.rem(me_x + k, nx),
+                    left_sem.at[u, me_x, team(k)],
+                    lax.rem(me_x + d, nx),
                 ).start()
 
         def forward_right(src, s):
@@ -268,13 +284,13 @@
                     left_u.at[to],
                     left_all.at[u, me_x, me_z],
                     sent_sem.at[0, u],
-                    left_sem.at[u, me_x, me_z],
+                    left_sem.at[u, me_x, team(k)],
                     to,
                 ).start()
                 return _
 
             lax.fori_loop(0, nz - 1, send, 0)
-            forward_left(left_u.at[me_z], me_z)
+            forward_left(left_u.at[me_z], me_z, nz - 1)
             left_all[u, me_x, me_z] = left_u[me_z]
 
         def send_right():
@@ -284,7 +300,7 @@
                     right_u.at[to],
                     right_in.at[u, me_z],
                     sent_sem.at[1, u],
-                    right_sem.at[u, me_z],
+                    right_sem.at[u, team(k)],
                     to,
                 ).start()
                 return _
@@ -302,10 +318,15 @@
             s = far_first(k)
             slot = left_all.at[u, me_x, s]
 
+            wait_team(
+                k,
+                lambda ref: copy_z(ref, ref, sent_sem.at[0, u], left_sem.at[u, me_x, team(k)], s),
+                2,
+            )
+
             @pl.when(k < nz - 1)
             def run():
-                copy_z(slot, slot, sent_sem.at[0, u], left_sem.at[u, me_x, s], s).wait_recv()
-                forward_left(slot, s)
+                forward_left(slot, s, k)
 
             store_rows(left_mat, me_x, s * geo.rows, left_all[u, me_x, s].astype(F32))
 
@@ -313,16 +334,17 @@
             s = far_first(k)
             for d in range(1, nx):
                 x = lax.rem(me_x + d, nx)
-                slot = left_all.at[u, x, s]
-                copy_x(slot, slot, sent_sem.at[2, u], left_sem.at[u, x, s], x).wait_recv()
+                wait_team(
+                    k,
+                    lambda ref: copy_x(ref, ref, sent_sem.at[2, u], left_sem.at[u, x, team(k)], x),
+                    3,
+                )
                 store_rows(left_mat, x, s * geo.rows, left_all[u, x, s].astype(F32))
 
         def wait_right(k, s):
-            slot = right_in.at[u, s]
-
-            @pl.when(k < nz - 1)
-            def run():
-                copy_z(slot, slot, sent_sem.at[1, u], right_sem.at[u, s], s).wait_recv()
+            wait_team(
+                k, lambda ref: copy_z(ref, ref, sent_sem.at[1, u], right_sem.at[u, team(k)], s), 2
+            )
 
         def block_row(base, r):
             return jnp.concatenate([product[h, pl.ds(base + r, 1), :] for h in range(2)], axis=0)
@@ -337,7 +359,7 @@
             @pl.when(k < nz - 1)
             def run():
                 copy_z(
-                    back_u.at[to], back_in.at[u, me_z], sent_sem.at[4, u], back_sem.at[u, me_z], to
+                    back_u.at[to], back_in.at[u, me_z], sent_sem.at[4, u], back_sem.at[u, team(k)], to
                 ).start()
 
         project(0, left_u)
@@ -440,21 +462,23 @@
         def take_back(k, _):
             s = far_first(k)
             slot = back_in.at[u, s]
-            copy_z(slot, slot, sent_sem.at[4, u], back_sem.at[u, s], s).wait_recv()
-            copy_c(slot, back_other.at[u, s], sent_sem.at[6, u], other_sem.at[u, s]).start()
+            wait_team(
+                k, lambda ref: copy_z(ref, ref, sent_sem.at[4, u], back_sem.at[u, team(k)], s), 2
+            )
+            copy_c(slot, back_other.at[u, s], sent_sem.at[6, u], other_sem.at[u, team(k)]).start()
             triangle[me_c, s] = back_in[u, s].astype(F32)
             return _
 
         copy_c(
-            back_u.at[me_z], back_other.at[u, me_z], sent_sem.at[6, u], other_sem.at[u, me_z]
+            back_u.at[me_z], back_other.at[u, me_z], sent_sem.at[6, u], other_sem.at[u, team(nz - 1)]
         ).start()
         triangle[me_c, me_z] = back_u[me_z].astype(F32)
         lax.fori_loop(0, nz - 1, take_back, 0)
 
         def take_other(k, _):
-            slot = back_other.at[u, k]
-            copy_c(slot, slot, sent_sem.at[6, u], other_sem.at[u, k]).wait_recv()
-            triangle[other_c, k] = back_other[u, k].astype(F32)
+            s = far_first(k)
+            wait_team(k, lambda ref: copy_c(ref, ref, sent_sem.at[6, u], other_sem.at[u, team(k)]), 3)
+            triangle[other_c, s] = back_other[u, s].astype(F32)
             return _
 
         lax.fori_loop(0, nz, take_other, 0)
@@ -551,11 +575,11 @@
             vmem((2, nz, *message), BF16),
             vmem((2, nz, *message), BF16),
             vmem((2, nz, *message), F32),
-            dma((2, nx, nz)),
-            dma((2, nz)),
+            dma((2, nx, nz // 4 + 1)),
+            dma((2, nz // 4 + 1)),
             dma((nx, geo.near)),
-            dma((2, nz)),
-            dma((2, nz)),
+            dma((2, nz // 4 + 1)),
+            dma((2, nz // 4 + 1)),
             dma((2, geo.extra)),
             dma((7, 2)),
             dma((6,)),

time: 175 us -> 178 us (1.017)
  Pallas kernels: 174 us -> 176 us
    pallas_call x1, Pallas kernels: 174 us -> 176 us  [per_device(): pl.pallas_call(functools.partial(kernel, geo, half), out_shape=jax.ShapeD...]
where the time goes in v6:
time: 178 us
  Pallas kernels  176 us (99%)
    pallas_call x1, Pallas kernels, per_device(): pl.pallas_call(functools.partial(kernel, geo, half), out_shape=jax.ShapeD...  176 us

profile of v6, /device:TPU:33, one launch (start us, length us, event | category | flops | bytes accessed | tf_op | source)
XLA Modules:
  0.0 177.9 jit_solution(12318667858698545014)
XLA Ops:
  0.0 176.1 %triangle_updates.1 = f32[12,64,96]{2,1,0:T(8,128)} custom-call(f32[12,64,96]{2,1,0:T(8,128)} %bitcast.6, s32[384]{0:T(512)} %flag_ref.1, f32[2,64]{1,0:T(2,128)} %gain_in_hbm.1, bf16[2,4,64,128]{3,2,1,0:T(8,128)(2,1)} %bitcast.7, bf16[2,64,128]{2,1,0:T(8,128)(2,1)} %bitcast.8, f32[2,64]{1,0:T(2,128)} %gain_out_hbm.1, bf16[2,64,128]{2,1,0:T(8,128)(2,1)} %bitcast.9), custom_call_target="tpu_custom_call" | custom-call | tf_op jit(solution)/shard_map/triangle_updates/pallas_call | solution.py:542
  176.1 1.8 copy.9

commit v7 on v3

--- a/solution.py
+++ b/solution.py
@@ -66,14 +66,11 @@
     half,
     pair_hbm,
     flag_ref,
-    gain_in_hbm,
     proj_hbm,
     gate_hbm,
-    gain_out_hbm,
     out_hbm,
     out_ref,
     pair_ref,
-    gains,
     proj_ref,
     gate_ref,
     out_weight_ref,
@@ -151,15 +148,12 @@
                 mat[lead, h, pl.ds(base + r, 1), :] = row[h : h + 1, :]
 
     lag = 8
-    wide = geo.width
 
     loads = [
         pltpu.make_async_copy(src, dst, load_sem.at[i])
         for i, (src, dst) in enumerate(
             [
                 (pair_hbm, pair_ref),
-                (gain_in_hbm, gains.at[0]),
-                (gain_out_hbm, gains.at[1]),
                 (proj_hbm, proj_ref),
                 (gate_hbm, gate_ref),
                 (out_hbm, out_weight_ref),
@@ -168,27 +162,16 @@
     ]
     for load in loads:
         load.start()
-    for load in loads[:3]:
+    for load in loads[:1]:
         load.wait()
-    for k in range(geo.blocks):
-        e, q = divmod(k, geo.pieces)
-        low = geo.spare * q
-        z_all[0, me_c, :, k * LANES : (k + 1) * LANES] = jnp.concatenate(
-            [pair_ref[k], pair_ref[geo.blocks + e, :, low : low + geo.spare]], axis=1
-        )
-    diagonal = lax.broadcasted_iota(jnp.int32, (half, half), 0) == lax.broadcasted_iota(
-        jnp.int32, (half, half), 1
-    )
-    columns = [
-        jnp.sum(jnp.where(diagonal, gains[kind, u : u + 1, :], 0.0), axis=1, keepdims=True)
-        for kind in range(2)
-        for u in range(2)
-    ]
-    lane = lax.broadcasted_iota(jnp.int32, (half, LANES), 1)
-    last = jnp.zeros((half, LANES), F32)
-    for i, column in enumerate(columns):
-        last = jnp.where(lane == i, column, last)
-    z_all[0, me_c, :, wide:] = last
+    for c in range(2):
+        own = slice(c * half, (c + 1) * half)
+        for k in range(geo.blocks):
+            e, q = divmod(k, geo.pieces)
+            low = geo.spare * q
+            z_all[0, c, :, k * LANES : (k + 1) * LANES] = jnp.concatenate(
+                [pair_ref[k, own, :], pair_ref[geo.blocks + e, own, low : low + geo.spare]], axis=1
+            )
 
     near_lane = lax.broadcasted_iota(jnp.int32, (1, LANES), 1)
     near_flags = jnp.zeros((1, LANES), F32)
@@ -201,30 +184,21 @@
             geo, lambda r: near_flags * row_flag[r], k
         )
 
-    for load in loads[3:]:
+    for load in loads[1:]:
         load.wait()
 
-    pl.semaphore_wait(barrier, nz - 1 + nx - 1 + 1)
-
-    def z_piece(u, i):
-        low = i * chunk
-        high = low + chunk + (LANES if u == 0 and i == geo.extra - 1 else 0)
-        part = z_all.at[u, me_c, :, low:high]
-        return copy_c(part, part, sent_sem.at[5, u], z_sem.at[u, i])
-
-    for i in reversed(range(geo.extra)):
-        z_piece(0, i).start()
+    def z_piece(i):
+        part = z_all.at[1, me_c, :, chunks[i]]
+        return copy_c(part, part, sent_sem.at[5, 0], z_sem.at[i])
 
     for u in range(2):
         left_u, right_u, back_u = left_out.at[u], right_out.at[u], back_out.at[u]
 
         for i in reversed(range(geo.extra)):
-            z_piece(u, i).wait_recv()
+            if u == 1:
+                z_piece(i).wait_recv()
             s = chunks[i]
-            if i == geo.extra - 1:
-                gain_in = jnp.concatenate(
-                    [z_all[0, c, :, wide + u : wide + u + 1] for c in range(2)], axis=0
-                )
+            gain_in = pair_ref[geo.rows, :, u : u + 1]
             z = jnp.concatenate([z_all[u, 0, :, s], z_all[u, 1, :, s]], axis=0)
             zn[:, s] = normed(z, gain_in)
 
@@ -341,6 +315,8 @@
                 ).start()
 
         project(0, left_u)
+        if u == 0:
+            pl.semaphore_wait(barrier, nz - 1 + nx - 1 + 1)
         send_left()
         project(2, right_u)
         send_right()
@@ -441,26 +417,26 @@
             s = far_first(k)
             slot = back_in.at[u, s]
             copy_z(slot, slot, sent_sem.at[4, u], back_sem.at[u, s], s).wait_recv()
-            copy_c(slot, back_other.at[u, s], sent_sem.at[6, u], other_sem.at[u, s]).start()
+            copy_c(slot, back_other.at[u, s], sent_sem.at[6, u], other_sem.at[u]).start()
             triangle[me_c, s] = back_in[u, s].astype(F32)
             return _
 
         copy_c(
-            back_u.at[me_z], back_other.at[u, me_z], sent_sem.at[6, u], other_sem.at[u, me_z]
+            back_u.at[me_z], back_other.at[u, me_z], sent_sem.at[6, u], other_sem.at[u]
         ).start()
         triangle[me_c, me_z] = back_u[me_z].astype(F32)
         lax.fori_loop(0, nz - 1, take_back, 0)
 
+        all_other = back_other.at[u]
+        copy_c(all_other, all_other, sent_sem.at[6, u], other_sem.at[u]).wait_recv()
+
         def take_other(k, _):
-            slot = back_other.at[u, k]
-            copy_c(slot, slot, sent_sem.at[6, u], other_sem.at[u, k]).wait_recv()
             triangle[other_c, k] = back_other[u, k].astype(F32)
             return _
 
         lax.fori_loop(0, nz, take_other, 0)
 
-        at = wide + 2 + u
-        gain_out = jnp.concatenate([z_all[0, c, :, at : at + 1] for c in range(2)], axis=0)
+        gain_out = pair_ref[geo.rows, :, 2 + u : 3 + u]
         for i in reversed(range(geo.extra)):
             s = chunks[i]
             values = jnp.concatenate(
@@ -471,7 +447,7 @@
             value = z_all[u, me_c, :, s] + gate[:, s] * change
             if u == 0:
                 z_all[1, me_c, :, s] = value
-                z_piece(1, i).start()
+                z_piece(i).start()
             else:
                 lane = lax.broadcasted_iota(jnp.int32, (half, LANES), 1)
                 row = jnp.zeros((half, LANES), F32)
@@ -483,7 +459,7 @@
                     row = jnp.where((lane >= low) & (lane < low + geo.spare), moved, row)
                 out_ref[geo.blocks + i] = row[:, : geo.cols]
 
-    any_sem = z_sem.at[0, 0]
+    any_sem = z_sem.at[0]
     for u in range(2):
         many = left_out.at[u, pl.ds(0, nz - 1)]
         copy_z(many, many, sent_sem.at[0, u], any_sem, me_z).wait_send()
@@ -496,9 +472,8 @@
         copy_c(every, every, sent_sem.at[6, u], any_sem).wait_send()
     away = left_out.at[0, pl.ds(0, nz - geo.near)]
     copy_x(away, away, sent_sem.at[3, 0], any_sem, me_x).wait_send()
-    for u in range(2):
-        part = z_all.at[u, me_c, :, : wide + (LANES if u == 0 else 0)]
-        copy_c(part, part, sent_sem.at[5, u], any_sem).wait_send()
+    part = z_all.at[1, me_c]
+    copy_c(part, part, sent_sem.at[5, 0], any_sem).wait_send()
 
 
 def per_device(
@@ -512,17 +487,19 @@
     dma = pltpu.SemaphoreType.DMA
     hbm = pl.BlockSpec(memory_space=pl.ANY)
     pair = jnp.swapaxes(pair, 0, 1)
+    gains = jnp.concatenate([norm_in_gain, norm_out_gain], axis=0).T
+    gains = jnp.pad(gains, ((0, 0), (0, geo.cols - gains.shape[1])))
+    pair = jnp.concatenate([pair, gains[None]], axis=0)
+    pair = lax.all_gather(pair, "gz", axis=1, tiled=True)
     proj_weight = jnp.swapaxes(proj_weight, 2, 3)
     gate_weight = jnp.swapaxes(gate_weight, 1, 2)
     out_weight = jnp.swapaxes(out_weight, 1, 2)
     result = pl.pallas_call(
         functools.partial(kernel, geo, half),
-        out_shape=jax.ShapeDtypeStruct(pair.shape, F32),
+        out_shape=jax.ShapeDtypeStruct((geo.rows, half, geo.cols), F32),
         in_specs=[
             hbm,
             pl.BlockSpec(memory_space=pltpu.SMEM),
-            hbm,
-            hbm,
             hbm,
             hbm,
             hbm,
@@ -530,12 +507,11 @@
         out_specs=pl.BlockSpec(memory_space=vmem),
         scratch_shapes=[
             vmem(pair.shape, F32),
-            vmem((2, *norm_in_gain.shape), F32),
             vmem(proj_weight.shape, BF16),
             vmem(gate_weight.shape, BF16),
             vmem(out_weight.shape, BF16),
             vmem((1, geo.width), F32),
-            vmem((2, 2, half, geo.width + LANES), F32),
+            vmem((2, 2, half, geo.width), F32),
             vmem((full, geo.width), BF16),
             vmem((half, geo.width), F32),
             vmem((half, geo.width), F32),
@@ -555,10 +531,10 @@
             dma((2, nz)),
             dma((nx, geo.near)),
             dma((2, nz)),
-            dma((2, nz)),
-            dma((2, geo.extra)),
+            dma((2,)),
+            dma((geo.extra,)),
             dma((7, 2)),
-            dma((6,)),
+            dma((4,)),
         ],
         compiler_params=pltpu.CompilerParams(
             collective_id=0, has_side_effects=True, vmem_limit_bytes=60 * 1024 * 1024
@@ -567,10 +543,8 @@
     )(
         pair,
         residue_mask,
-        norm_in_gain,
         proj_weight,
         gate_weight,
-        norm_out_gain,
         out_weight,
     )
     return jnp.swapaxes(result, 0, 1)

time: 175 us -> 177 us (1.011)
  Pallas kernels: 174 us -> 129 us
  blocking collectives: 0 us -> 43.7 us
    pallas_call x1, Pallas kernels: 174 us -> 129 us  [per_device(): pl.pallas_call(functools.partial(kernel, geo, half), out_shape=jax.ShapeD...]
    all_gather x0 -> x1, blocking collectives: none -> 43.7 us  [per_device(): pair = lax.all_gather(pair, 'gz', axis=1, tiled=True)]
where the time goes in v7:
time: 177 us; the launch traced here: 176 us
  Pallas kernels  129 us (73%)
  blocking collectives  43.7 us (25%)
  local copies, waits for them, and re-layouts  2.57 us (1%)
    pallas_call x1, Pallas kernels, per_device(): pl.pallas_call(functools.partial(kernel, geo, half), out_shape=jax.ShapeD...  129 us
    all_gather x1, blocking collectives, per_device(): pair = lax.all_gather(pair, 'gz', axis=1, tiled=True)  43.7 us

profile of v7, /device:TPU:33, one launch (start us, length us, event | category | flops | bytes accessed | tf_op | source)
XLA Modules:
  0.0 176.3 jit_solution(15365293803189874860)
XLA Ops:
  0.0 0.0 copy-start.1
  0.0 0.0 copy-start
  0.0 0.7 copy-done.1
  0.7 0.0 copy-done
  0.7 0.1 copy.10
  0.8 1.0 pad_maximum_fusion
  1.9 43.7 %all_gather.3.pair_hbm = f32[13,128,96]{2,1,0:T(8,128)} all-gather(f32[13,64,96]{2,1,0:T(8,128)S(1)} %pad_maximum_fusion), channel_id=1, replica_groups=mesh['groups'=2,'gx'=32,'gy'=4,'gz'=2] {'gz'}, dimensions={1}, use_global_device_ids=true | all-gather | bytes 958464 | tf_op jit(solution)/shard_map/all_gather | solution.py:493
  45.5 129.0 %triangle_updates.1 = f32[12,64,96]{2,1,0:T(8,128)} custom-call(f32[13,128,96]{2,1,0:T(8,128)} %all_gather.3.pair_hbm, s32[384]{0:T(512)} %flag_ref.1, bf16[2,4,64,128]{3,2,1,0:T(8,128)(2,1)} %bitcast.11, bf16[2,64,128]{2,1,0:T(8,128)(2,1)} %bitcast.12, bf16[2,64,128]{2,1,0:T(8,128)(2,1)} %bitcast.13), custom_call_target="tpu_custom_call" | custom-call | tf_op jit(solution)/shard_map/triangle_updates/pallas_call | solution.py:497
  174.5 1.8 %copy.12 = f32[64,12,96]{2,0,1:T(8,128)} copy(f32[64,12,96]{2,0,1:T(8,128)} %bitcast.8) | data formatting | bytes 589824
  (2 shorter events, 0.0 us)
Async XLA Ops:
  0.0 0.7 copy-start.1
  0.0 0.7 copy-start

commit v8 on v7

--- a/solution.py
+++ b/solution.py
@@ -147,6 +147,7 @@
             for h in range(2):
                 mat[lead, h, pl.ds(base + r, 1), :] = row[h : h + 1, :]
 
+    group = 4
     lag = 8
 
     loads = [
@@ -272,6 +273,9 @@
                     jnp.dot(gate_ref[u], zn[:, s], preferred_element_type=F32)
                 )
 
+        def left_base(k, s):
+            return (k if u == 0 else s) * geo.rows
+
         def take_left(k):
             s = far_first(k)
             slot = left_all.at[u, me_x, s]
@@ -281,7 +285,7 @@
                 copy_z(slot, slot, sent_sem.at[0, u], left_sem.at[u, me_x, s], s).wait_recv()
                 forward_left(slot, s)
 
-            store_rows(left_mat, me_x, s * geo.rows, left_all[u, me_x, s].astype(F32))
+            store_rows(left_mat, me_x, left_base(k, s), left_all[u, me_x, s].astype(F32))
 
         def take_left_x(k):
             s = far_first(k)
@@ -289,7 +293,7 @@
                 x = lax.rem(me_x + d, nx)
                 slot = left_all.at[u, x, s]
                 copy_x(slot, slot, sent_sem.at[2, u], left_sem.at[u, x, s], x).wait_recv()
-                store_rows(left_mat, x, s * geo.rows, left_all[u, x, s].astype(F32))
+                store_rows(left_mat, x, left_base(k, s), left_all[u, x, s].astype(F32))
 
         def wait_right(k, s):
             slot = right_in.at[u, s]
@@ -303,7 +307,7 @@
 
         def send_back(k):
             to = far_first(k)
-            base = to * geo.rows
+            base = left_base(k, to)
             for b in range(geo.blocks):
                 value = block_of(geo, functools.partial(block_row, base), b)
                 back_u[to, :, b * LANES : (b + 1) * LANES] = value.astype(BF16)
@@ -314,43 +318,18 @@
                     back_u.at[to], back_in.at[u, me_z], sent_sem.at[4, u], back_sem.at[u, me_z], to
                 ).start()
 
-        project(0, left_u)
         if u == 0:
+            project(2, right_u)
             pl.semaphore_wait(barrier, nz - 1 + nx - 1 + 1)
-        send_left()
-        project(2, right_u)
-        send_right()
-        if u == 0:
+            send_right()
             forward_right(right_u.at[me_z], me_z)
-        open_gate()
-
-        def take_lefts(k, _):
-            take_left(k)
-
-            @pl.when(k >= lag)
-            def run():
-                take_left_x(k - lag)
-
-            return _
-
-        lax.fori_loop(0, nz, take_lefts, 0)
-
-        def take_right_x(k):
-            s = far_first(k)
-            at = s % geo.near
-
-            @pl.when(s // geo.near == me_x)
-            def run():
-                for d in range(1, nx):
-                    x = lax.rem(me_x + d, nx)
-                    slot = right_all.at[x, at]
-                    copy_x(slot, slot, sent_sem.at[3, 0], right_x_sem.at[x, at], x).wait_recv()
-                    store_rows(right_mat, x, at * geo.rows, right_all[x, at].astype(F32))
-
-        def take_right(k, _):
-            s = far_first(k)
-            wait_right(k, s)
-            if u == 0:
+            project(0, left_u)
+            send_left()
+            open_gate()
+
+            def take_right(k, _):
+                s = far_first(k)
+                wait_right(k, s)
 
                 @pl.when(k < nz - 1)
                 def run():
@@ -362,40 +341,94 @@
                         right_mat, me_x, (s % geo.near) * geo.rows, right_in[0, s].astype(F32)
                     )
 
+                return _
+
+            lax.fori_loop(0, nz, take_right, 0)
+
+            def take_group(g):
+                def take(i, _):
+                    take_left(g * group + i)
+                    return _
+
+                lax.fori_loop(0, group, take, 0)
+
+            take_group(0)
+
+            for d in range(1, nx):
+                x = lax.rem(me_x + d, nx)
+
+                def take_right_x(k, _):
+                    slot = right_all.at[x, k]
+                    copy_x(slot, slot, sent_sem.at[3, 0], right_x_sem.at[x, k], x).wait_recv()
+                    store_rows(right_mat, x, k * geo.rows, right_all[x, k].astype(F32))
+                    return _
+
+                lax.fori_loop(0, geo.near, take_right_x, 0)
+            take_group(1)
+
+            tall = group * geo.rows
+
+            def work(g, _):
+                @pl.when(g < nz // group - 2)
+                def run():
+                    take_group(g + 2)
+
+                def take_x(i, _):
+                    take_left_x(g * group + i)
+                    return _
+
+                lax.fori_loop(0, group, take_x, 0)
+                rows = pl.ds(pl.multiple_of(g * tall, tall), tall)
+                for h in range(2):
+                    total = jnp.zeros((tall, geo.cols), F32)
+                    for x in range(nx):
+                        total += lax.dot_general(
+                            left_mat[x, h, rows, :].astype(BF16),
+                            right_mat[x, h, : geo.cols, :].astype(BF16),
+                            (((1,), (1,)), ((), ())),
+                            preferred_element_type=F32,
+                        )
+                    product[h, rows, : geo.cols] = total
+
+                def send(i, _):
+                    send_back(g * group + i)
+                    return _
+
+                lax.fori_loop(0, group, send, 0)
+                return _
+
+            lax.fori_loop(0, nz // group, work, 0)
+        else:
+            project(0, left_u)
+            send_left()
+            project(2, right_u)
+            send_right()
+            open_gate()
+
+            def take_lefts(k, _):
+                take_left(k)
+
                 @pl.when(k >= lag)
-                def run_x():
-                    take_right_x(k - lag)
-
-            else:
+                def run():
+                    take_left_x(k - lag)
+
+                return _
+
+            lax.fori_loop(0, nz, take_lefts, 0)
+
+            def take_right(k, _):
+                s = far_first(k)
+                wait_right(k, s)
                 store_rows(right_mat, 0, s * geo.rows, right_in[1, s].astype(F32))
 
-            @pl.when(k < lag)
-            def run_left():
-                take_left_x(nz - lag + k)
-
-            return _
-
-        lax.fori_loop(0, nz, take_right, 0)
-
-        if u == 0:
-
-            def take_last(k, _):
-                take_right_x(k)
+                @pl.when(k < lag)
+                def run():
+                    take_left_x(nz - lag + k)
+
                 return _
 
-            lax.fori_loop(nz - lag, nz, take_last, 0)
-
-            for h in range(2):
-                total = jnp.zeros((geo.res, geo.cols), F32)
-                for x in range(nx):
-                    total += lax.dot_general(
-                        left_mat[x, h].astype(BF16),
-                        right_mat[x, h, : geo.cols, :].astype(BF16),
-                        (((1,), (1,)), ((), ())),
-                        preferred_element_type=F32,
-                    )
-                product[h, :, : geo.cols] = total
-        else:
+            lax.fori_loop(0, nz, take_right, 0)
+
             for h in range(2):
                 right = right_mat[0, h].astype(BF16)
                 for x in range(nx):
@@ -407,11 +440,11 @@
                     )
                     product[h, geo.cols * x : geo.cols * (x + 1), :] = part[: geo.cols, :]
 
-        def send(k, _):
-            send_back(k)
-            return _
-
-        lax.fori_loop(0, nz, send, 0)
+            def send(k, _):
+                send_back(k)
+                return _
+
+            lax.fori_loop(0, nz, send, 0)
 
         def take_back(k, _):
             s = far_first(k)

time: 177 us -> 168 us (0.949)
  Pallas kernels: 129 us -> 121 us
    pallas_call x1, Pallas kernels: 129 us -> 121 us  [per_device(): pl.pallas_call(functools.partial(kernel, geo, half), out_shape=jax.ShapeD...]
where the time goes in v8:
time: 168 us
  Pallas kernels  121 us (72%)
  blocking collectives  43.7 us (26%)
  local copies, waits for them, and re-layouts  2.57 us (2%)
    pallas_call x1, Pallas kernels, per_device(): pl.pallas_call(functools.partial(kernel, geo, half), out_shape=jax.ShapeD...  121 us
    all_gather x1, blocking collectives, per_device(): pair = lax.all_gather(pair, 'gz', axis=1, tiled=True)  43.7 us

profile of v8, /device:TPU:33, one launch (start us, length us, event | category | flops | bytes accessed | tf_op | source)
XLA Modules:
  0.0 168.0 jit_solution(5743904624297889203)
XLA Ops:
  0.0 0.0 copy-start.1
  0.0 0.0 copy-start
  0.0 0.7 copy-done.1
  0.7 0.0 copy-done
  0.7 0.1 copy.10
  0.8 1.0 pad_maximum_fusion
  1.9 43.7 %all_gather.3.pair_hbm = f32[13,128,96]{2,1,0:T(8,128)} all-gather(f32[13,64,96]{2,1,0:T(8,128)S(1)} %pad_maximum_fusion), channel_id=1, replica_groups=mesh['groups'=2,'gx'=32,'gy'=4,'gz'=2] {'gz'}, dimensions={1}, use_global_device_ids=true | all-gather | bytes 958464 | tf_op jit(solution)/shard_map/all_gather | solution.py:526
  45.5 120.7 %triangle_updates.1 = f32[12,64,96]{2,1,0:T(8,128)} custom-call(f32[13,128,96]{2,1,0:T(8,128)} %all_gather.3.pair_hbm, s32[384]{0:T(512)} %flag_ref.1, bf16[2,4,64,128]{3,2,1,0:T(8,128)(2,1)} %bitcast.11, bf16[2,64,128]{2,1,0:T(8,128)(2,1)} %bitcast.12, bf16[2,64,128]{2,1,0:T(8,128)(2,1)} %bitcast.13), custom_call_target="tpu_custom_call" | custom-call | tf_op jit(solution)/shard_map/triangle_updates/pallas_call | solution.py:530
  166.2 1.8 %copy.12 = f32[64,12,96]{2,0,1:T(8,128)} copy(f32[64,12,96]{2,0,1:T(8,128)} %bitcast.8) | data formatting | bytes 589824
  (2 shorter events, 0.0 us)
Async XLA Ops:
  0.0 0.7 copy-start.1
  0.0 0.7 copy-start

commit v9 on v8

--- a/solution.py
+++ b/solution.py
@@ -285,15 +285,18 @@
                 copy_z(slot, slot, sent_sem.at[0, u], left_sem.at[u, me_x, s], s).wait_recv()
                 forward_left(slot, s)
 
-            store_rows(left_mat, me_x, left_base(k, s), left_all[u, me_x, s].astype(F32))
-
         def take_left_x(k):
             s = far_first(k)
             for d in range(1, nx):
                 x = lax.rem(me_x + d, nx)
                 slot = left_all.at[u, x, s]
                 copy_x(slot, slot, sent_sem.at[2, u], left_sem.at[u, x, s], x).wait_recv()
-                store_rows(left_mat, x, left_base(k, s), left_all[u, x, s].astype(F32))
+            value = jnp.concatenate([left_all[u, x, s].astype(F32) for x in range(nx)], axis=0)
+            for r, row in enumerate(rows_of(geo, value)):
+                at = pl.ds(left_base(k, s) + r, 1)
+                for x in range(nx):
+                    for h in range(2):
+                        left_mat[x, h, at, :] = row[2 * x + h : 2 * x + h + 1, :]
 
         def wait_right(k, s):
             slot = right_in.at[u, s]

time: 168 us -> 169 us (level)
  no operation moved by 1% of the time
where the time goes in v9:
time: 169 us
  Pallas kernels  121 us (72%)
  blocking collectives  43.7 us (26%)
  local copies, waits for them, and re-layouts  2.57 us (2%)
    pallas_call x1, Pallas kernels, per_device(): pl.pallas_call(functools.partial(kernel, geo, half), out_shape=jax.ShapeD...  121 us
    all_gather x1, blocking collectives, per_device(): pair = lax.all_gather(pair, 'gz', axis=1, tiled=True)  43.7 us

profile of v9, /device:TPU:33, one launch (start us, length us, event | category | flops | bytes accessed | tf_op | source)
XLA Modules:
  0.0 168.8 jit_solution(466943916079147559)
XLA Ops:
  0.0 0.0 copy-start.1
  0.0 0.0 copy-start
  0.0 0.7 copy-done.1
  0.7 0.0 copy-done
  0.7 0.1 copy.10
  0.8 1.0 pad_maximum_fusion
  1.9 43.7 %all_gather.3.pair_hbm = f32[13,128,96]{2,1,0:T(8,128)} all-gather(f32[13,64,96]{2,1,0:T(8,128)S(1)} %pad_maximum_fusion), channel_id=1, replica_groups=mesh['groups'=2,'gx'=32,'gy'=4,'gz'=2] {'gz'}, dimensions={1}, use_global_device_ids=true | all-gather | bytes 958464 | tf_op jit(solution)/shard_map/all_gather | solution.py:529
  45.5 121.5 %triangle_updates.1 = f32[12,64,96]{2,1,0:T(8,128)} custom-call(f32[13,128,96]{2,1,0:T(8,128)} %all_gather.3.pair_hbm, s32[384]{0:T(512)} %flag_ref.1, bf16[2,4,64,128]{3,2,1,0:T(8,128)(2,1)} %bitcast.11, bf16[2,64,128]{2,1,0:T(8,128)(2,1)} %bitcast.12, bf16[2,64,128]{2,1,0:T(8,128)(2,1)} %bitcast.13), custom_call_target="tpu_custom_call" | custom-call | tf_op jit(solution)/shard_map/triangle_updates/pallas_call | solution.py:533
  167.0 1.8 %copy.12 = f32[64,12,96]{2,0,1:T(8,128)} copy(f32[64,12,96]{2,0,1:T(8,128)} %bitcast.8) | data formatting | bytes 589824
  (2 shorter events, 0.0 us)
Async XLA Ops:
  0.0 0.7 copy-start.1
  0.0 0.7 copy-start

commit v10 on v8

--- a/solution.py
+++ b/solution.py
@@ -110,10 +110,12 @@
 
     barrier = pltpu.get_barrier_semaphore()
 
+    def far_first(k):
+        m = (k + 1) // 2
+        return lax.rem(me_z + nz // 2 + m * (1 - 2 * (k % 2)), nz)
+
     def signal_z(k, _):
-        pl.semaphore_signal(
-            barrier, inc=1, device_id={"gx": lax.rem(me_z + 1 + k, nz)}, device_id_type=MESH
-        )
+        pl.semaphore_signal(barrier, inc=1, device_id={"gx": far_first(k)}, device_id_type=MESH)
         return _
 
     lax.fori_loop(0, nz - 1, signal_z, 0)
@@ -122,10 +124,6 @@
             barrier, inc=1, device_id={"gy": lax.rem(me_x + k, nx)}, device_id_type=MESH
         )
     pl.semaphore_signal(barrier, inc=1, device_id={"gz": other_c}, device_id_type=MESH)
-
-    def far_first(k):
-        m = (k + 1) // 2
-        return lax.rem(me_z + nz // 2 + m * (1 - 2 * (k % 2)), nz)
 
     def copy_z(src, dst, send, recv, to):
         return pltpu.make_async_remote_copy(

time: 168 us -> 168 us (level)
  no operation moved by 1% of the time
where the time goes in v10:
time: 168 us; the launch traced here: 167 us
  Pallas kernels  120 us (71%)
  blocking collectives  43.7 us (26%)
  local copies, waits for them, and re-layouts  2.57 us (2%)
    pallas_call x1, Pallas kernels, per_device(): pl.pallas_call(functools.partial(kernel, geo, half), out_shape=jax.ShapeD...  120 us
    all_gather x1, blocking collectives, per_device(): pair = lax.all_gather(pair, 'gz', axis=1, tiled=True)  43.7 us

profile of v10, /device:TPU:33, one launch (start us, length us, event | category | flops | bytes accessed | tf_op | source)
XLA Modules:
  0.0 167.3 jit_solution(6759020787829791919)
XLA Ops:
  0.0 0.0 copy-start.1
  0.0 0.0 copy-start
  0.0 0.7 copy-done.1
  0.7 0.0 copy-done
  0.7 0.1 copy.10
  0.8 1.0 pad_maximum_fusion
  1.9 43.7 %all_gather.3.pair_hbm = f32[13,128,96]{2,1,0:T(8,128)} all-gather(f32[13,64,96]{2,1,0:T(8,128)S(1)} %pad_maximum_fusion), channel_id=1, replica_groups=mesh['groups'=2,'gx'=32,'gy'=4,'gz'=2] {'gz'}, dimensions={1}, use_global_device_ids=true | all-gather | bytes 958464 | tf_op jit(solution)/shard_map/all_gather | solution.py:524
  45.5 120.0 %triangle_updates.1 = f32[12,64,96]{2,1,0:T(8,128)} custom-call(f32[13,128,96]{2,1,0:T(8,128)} %all_gather.3.pair_hbm, s32[384]{0:T(512)} %flag_ref.1, bf16[2,4,64,128]{3,2,1,0:T(8,128)(2,1)} %bitcast.11, bf16[2,64,128]{2,1,0:T(8,128)(2,1)} %bitcast.12, bf16[2,64,128]{2,1,0:T(8,128)(2,1)} %bitcast.13), custom_call_target="tpu_custom_call" | custom-call | tf_op jit(solution)/shard_map/triangle_updates/pallas_call | solution.py:528
  165.5 1.8 %copy.12 = f32[64,12,96]{2,0,1:T(8,128)} copy(f32[64,12,96]{2,0,1:T(8,128)} %bitcast.8) | data formatting | bytes 589824
  (2 shorter events, 0.0 us)
Async XLA Ops:
  0.0 0.7 copy-start.1
  0.0 0.7 copy-start
